TPU v7x, 512 devices: a whole 4x4x16 slice. The times are simulated.
512 devices in a mesh: ctx: 64 (over z, y), tp: 8 (over x, core).
Axes of the slice: x: 4, y: 4, z: 16, core: 2. Of those that a mesh axis runs over, the one named last changes fastest.
Arguments:
- rotated_asking_vectors: bfloat16 [2, 2048, 64, 128], P(None, ('ctx', 'tp')), may hold values from -6 to 6
- rotated_match_vectors: bfloat16 [2, 2048, 8, 128], P(None, ('ctx', 'tp')), may hold values from -6 to 6
- content_vectors: bfloat16 [2, 2048, 8, 128], P(None, ('ctx', 'tp')), may hold values from -6 to 6
- result_cotangent: bfloat16 [2, 2048, 64, 128], P(None, ('ctx', 'tp')), may hold values from -6 to 6
Outputs:
- attended: bfloat16 [2, 2048, 64, 128], P(None, ('ctx', 'tp'))
- grad_query: bfloat16 [2, 2048, 64, 128], P(None, ('ctx', 'tp'))
- grad_key: bfloat16 [2, 2048, 8, 128], P(None, ('ctx', 'tp'))
- grad_value: bfloat16 [2, 2048, 8, 128], P(None, ('ctx', 'tp'))
All inputs are finite; a program needn't handle non-finite values.
Results may differ from a plain program's by a relative error of at most 0.002.
Values may be sent and summed in bfloat16 or wider, within the bound.
A program may use at most 64 MiB of HBM per device.

v0:
```python
from functools import partial

import jax
import jax.numpy as jnp
from jax import lax
from jax.sharding import Mesh
from jax.sharding import PartitionSpec as P

CTX = ("ctx_0", "ctx_1")
CTX_TP = ("ctx_0", "ctx_1", "tp")


masked_score = -1e30


def gather_axes(value, axes, dim):
    for axis in reversed(axes):
        value = lax.all_gather(value, axis, axis=dim, tiled=True)
    return value


def folded(value, axes, dim, absorb, carry):
    everything = jax.tree.map(lambda part: gather_axes(part, axes, dim), value)
    return absorb(carry, everything, jnp.int32(0))


def cut_along(value, dim, size):
    lengths = value.shape
    tiles = value.reshape(*lengths[:dim], size, lengths[dim] // size, *lengths[dim + 1 :])
    return jnp.moveaxis(tiles, dim, 0)


def sum_packed(arrays, axis, dims):
    size = lax.axis_size(axis)
    tiles = [cut_along(a, dim, size) for a, dim in zip(arrays, dims)]
    lines = jnp.concatenate([b.reshape(size, -1) for b in tiles], axis=1)
    flat, at, finished = lax.psum_scatter(lines, axis, tiled=True)[0], 0, []
    for b in tiles:
        part = b[0]
        finished.append(flat[at : at + part.size].reshape(part.shape))
        at += part.size
    return tuple(finished)


def as_sent(value):
    def short(part):
        return part.astype(jnp.bfloat16) if part.dtype == jnp.float32 else part

    return jax.tree.map(short, value)


def add_rows(totals, piece, first_row):
    current = lax.dynamic_slice_in_dim(totals, first_row, piece.shape[0], 0)
    return lax.dynamic_update_slice_in_dim(totals, current + piece, first_row, 0)


def causal_scores(work_query, key_piece, first_row, positions, softmax_scale):
    piece_len = key_piece.shape[0]
    scores = (
        jnp.einsum("tkgd,nkd->tkgn", work_query, key_piece, preferred_element_type=jnp.float32)
        * softmax_scale
    )
    key_position = first_row + jnp.arange(piece_len, dtype=jnp.int32)
    allowed = (key_position[None, :] <= positions[:, None])[:, None, None, :]
    return (jnp.where(allowed, scores, masked_score), allowed)


def forward_step(state_now, pieces, first_row, work_query, positions, softmax_scale):
    key_piece, value_piece = pieces

    def update(state_in):
        weighted, run_max, run_sum = state_in
        scores, allowed = causal_scores(work_query, key_piece, first_row, positions, softmax_scale)
        new_max = jnp.maximum(run_max, jnp.max(scores, axis=-1))
        weights = jnp.where(allowed, jnp.exp(scores - new_max[..., None]), 0.0)
        factor = jnp.exp(run_max - new_max)
        weighted = weighted * factor[..., None] + jnp.einsum(
            "tkgn,nkd->tkgd",
            weights,
            value_piece.astype(jnp.float32),
            precision=lax.Precision.HIGHEST,
        )
        run_sum = run_sum * factor + jnp.sum(weights, axis=-1)
        return (weighted, new_max, run_sum)

    return lax.cond(first_row <= jnp.max(positions), update, lambda state_in: state_in, state_now)


def backward_step(
    state_now,
    pieces,
    first_row,
    work_query,
    expanded_asking_vectors,
    work_grad,
    expanded_cotangent,
    log_norm,
    row_delta,
    positions,
    softmax_scale,
):
    key_piece, value_piece = pieces

    def update(state_in):
        query_total, key_total, value_total = state_in
        scores, allowed = causal_scores(work_query, key_piece, first_row, positions, softmax_scale)
        probabilities = jnp.where(allowed, jnp.exp(scores - log_norm[..., None]), 0.0)
        prob_grad = jnp.einsum(
            "tkgd,nkd->tkgn", work_grad, value_piece, preferred_element_type=jnp.float32
        )
        dscore = probabilities * (prob_grad - row_delta[..., None])
        query_total = query_total + softmax_scale * jnp.einsum(
            "tkgn,nkd->tkgd", dscore, key_piece.astype(jnp.float32), precision=lax.Precision.HIGHEST
        )
        key_term = softmax_scale * jnp.einsum(
            "tkgn,tkgd->nkd", dscore, expanded_asking_vectors, precision=lax.Precision.HIGHEST
        )
        value_term = jnp.einsum(
            "tkgn,tkgd->nkd", probabilities, expanded_cotangent, precision=lax.Precision.HIGHEST
        )
        return (
            query_total,
            add_rows(key_total, key_term, first_row),
            add_rows(value_total, value_term, first_row),
        )

    return lax.cond(first_row <= jnp.max(positions), update, lambda state_in: state_in, state_now)


def on_device(rotated_asking_vectors, rotated_match_vectors, content_vectors, result_cotangent):
    query_heads, key_heads, value_heads, grad_heads = (
        lax.all_to_all(rotated_asking_vectors, "tp", split_axis=2, concat_axis=1, tiled=True),
        lax.all_to_all(rotated_match_vectors, "tp", split_axis=2, concat_axis=1, tiled=True),
        lax.all_to_all(content_vectors, "tp", split_axis=2, concat_axis=1, tiled=True),
        lax.all_to_all(result_cotangent, "tp", split_axis=2, concat_axis=1, tiled=True),
    )
    layer_count, tok_rows, head_count, head_depth = query_heads.shape
    kv_heads = key_heads.shape[2]
    group_size = head_count // kv_heads
    ctx_count = lax.axis_size(CTX)
    ctx_rank = lax.axis_index(CTX)
    softmax_scale = head_depth ** (-0.5)
    total_rows = ctx_count * tok_rows
    own_rows = ctx_rank * tok_rows + jnp.arange(tok_rows, dtype=jnp.int32)
    work_queries, work_grads, positions = (query_heads, grad_heads, own_rows)
    attended_list, query_grads, key_parts, value_parts = ([], [], [], [])
    lead_shape = (tok_rows, kv_heads, group_size)
    for depth_position in range(layer_count):
        work_query = work_queries[depth_position].reshape(lead_shape + (head_depth,))
        work_grad = work_grads[depth_position].reshape(lead_shape + (head_depth,))
        forward_init = (
            jnp.zeros(lead_shape + (head_depth,), jnp.float32),
            jnp.full(lead_shape, masked_score, jnp.float32),
            jnp.zeros(lead_shape, jnp.float32),
        )
        forward_fn = partial(
            forward_step, work_query=work_query, positions=positions, softmax_scale=softmax_scale
        )
        weighted, run_max, run_sum = folded(
            (key_heads[depth_position], value_heads[depth_position]),
            CTX,
            0,
            forward_fn,
            forward_init,
        )
        attended_now = (weighted / run_sum[..., None]).astype(jnp.bfloat16)
        log_norm = run_max + jnp.log(run_sum)
        saved_out = lax.optimization_barrier(attended_now).astype(jnp.float32)
        expanded_cotangent = work_grad.astype(jnp.float32)
        row_delta = jnp.sum(expanded_cotangent * saved_out, axis=-1)
        expanded_asking_vectors = work_query.astype(jnp.float32)
        backward_init = (
            jnp.zeros(lead_shape + (head_depth,), jnp.float32),
            jnp.zeros((total_rows, kv_heads, head_depth), jnp.float32),
            jnp.zeros((total_rows, kv_heads, head_depth), jnp.float32),
        )
        backward_fn = partial(
            backward_step,
            work_query=work_query,
            expanded_asking_vectors=expanded_asking_vectors,
            work_grad=work_grad,
            expanded_cotangent=expanded_cotangent,
            log_norm=log_norm,
            row_delta=row_delta,
            positions=positions,
            softmax_scale=softmax_scale,
        )
        query_total, key_total, value_total = folded(
            (key_heads[depth_position], value_heads[depth_position]),
            CTX,
            0,
            backward_fn,
            backward_init,
        )
        attended_list.append(attended_now.reshape(tok_rows, head_count, head_depth))
        query_grads.append(
            query_total.astype(jnp.bfloat16).reshape(tok_rows, head_count, head_depth)
        )
        key_parts.append(key_total)
        value_parts.append(value_total)
    key_sum, value_sum = sum_packed((jnp.stack(key_parts), jnp.stack(value_parts)), CTX, (1, 1))
    attended = jnp.stack(attended_list)
    grad_query = jnp.stack(query_grads)
    return (
        lax.all_to_all(as_sent(attended), "tp", split_axis=1, concat_axis=2, tiled=True).astype(
            attended.dtype
        ),
        lax.all_to_all(as_sent(grad_query), "tp", split_axis=1, concat_axis=2, tiled=True).astype(
            grad_query.dtype
        ),
        lax.all_to_all(key_sum.astype(jnp.bfloat16), "tp", split_axis=1, concat_axis=2, tiled=True),
        lax.all_to_all(
            value_sum.astype(jnp.bfloat16), "tp", split_axis=1, concat_axis=2, tiled=True
        ),
    )


def solution(mesh):
    torus = Mesh(mesh.devices.reshape(16, 4, mesh.shape["tp"]), ("ctx_0", "ctx_1", "tp"))
    placed = (
        P(None, CTX_TP, None, None),
        P(None, CTX_TP, None, None),
        P(None, CTX_TP, None, None),
        P(None, CTX_TP, None, None),
    )
    return jax.shard_map(
        on_device,
        mesh=torus,
        in_specs=placed,
        out_specs=(
            P(None, CTX_TP, None, None),
            P(None, CTX_TP, None, None),
            P(None, CTX_TP, None, None),
            P(None, CTX_TP, None, None),
        ),
        check_vma=False,
    )
```

profile of v0, /device:TPU:1, one launch (start us, length us, event | category | flops | bytes accessed | tf_op | source)
XLA Modules:
  0.0 627.3 jit_solution(9293795545428458742)
XLA Ops:
  2.0 10.1 %all-to-all-start = ((bf16[2,4,8,128]{3,1,0,2:T(4,128)(2,1)}), bf16[2,4,8,128]{3,1,0,2:T(4,128)(2,1)S(1)}, u32[]{:S(2)}, u32[]{:S(2)}) async-start(bf16[2,4,8,128]{3,1,0,2:T(4,128)(2,1)} %copy.44), calls=%async_computation | async-start | bytes 32768 | tf_op jit(solution)/shard_map/all_to_all | solution.py:133
  19.3 4.8 all-to-all-start.2
  24.2 4.6 all-to-all-done.2
  28.8 4.0 all-to-all-start.1
  32.8 9.2 %all_gather.38 = bf16[128,1,128]{2,0,1:T(8,128)(2,1)S(1)} all-gather(bf16[32,1,128]{2,0,1:T(8,128)(2,1)S(1)} %bitcast.353), channel_id=1, replica_groups=mesh['ctx_0'=16,'ctx_1'=4,'tp'=8] {'ctx_1'}, dimensions={0}, use_global_device_ids=true | all-gather | bytes 40960 | tf_op jit(solution)/shard_map/all_gather | solution.py:18
  42.0 8.9 %all_gather.34 = bf16[128,1,128]{2,0,1:T(8,128)(2,1)S(1)} all-gather(bf16[32,1,128]{2,0,1:T(8,128)(2,1)S(1)} %bitcast.352), channel_id=1, replica_groups=mesh['ctx_0'=16,'ctx_1'=4,'tp'=8] {'ctx_1'}, dimensions={0}, use_global_device_ids=true | all-gather | bytes 40960 | tf_op jit(solution)/shard_map/all_gather | solution.py:18
  50.9 8.9 %all_gather.36 = bf16[128,1,128]{2,0,1:T(8,128)(2,1)S(1)} all-gather(bf16[32,1,128]{2,0,1:T(8,128)(2,1)S(1)} %bitcast.351), channel_id=1, replica_groups=mesh['ctx_0'=16,'ctx_1'=4,'tp'=8] {'ctx_1'}, dimensions={0}, use_global_device_ids=true | all-gather | bytes 40960 | tf_op jit(solution)/shard_map/all_gather | solution.py:18
  59.8 8.9 %all_gather.32 = bf16[128,1,128]{2,0,1:T(8,128)(2,1)S(1)} all-gather(bf16[32,1,128]{2,0,1:T(8,128)(2,1)S(1)} %bitcast.350), channel_id=1, replica_groups=mesh['ctx_0'=16,'ctx_1'=4,'tp'=8] {'ctx_1'}, dimensions={0}, use_global_device_ids=true | all-gather | bytes 40960 | tf_op jit(solution)/shard_map/all_gather | solution.py:18
  68.8 27.4 %all_gather.33 = bf16[2048,1,128]{2,0,1:T(8,128)(2,1)S(1)} all-gather(bf16[128,1,128]{2,0,1:T(8,128)(2,1)S(1)} %all_gather.32), channel_id=1, replica_groups=mesh['ctx_0'=16,'ctx_1'=4,'tp'=8] {'ctx_0'}, dimensions={0}, use_global_device_ids=true | all-gather | bytes 557056 | tf_op jit(solution)/shard_map/all_gather | solution.py:18
  96.2 22.6 %all_gather.37 = bf16[2048,1,128]{2,0,1:T(8,128)(2,1)S(1)} all-gather(bf16[128,1,128]{2,0,1:T(8,128)(2,1)S(1)} %all_gather.36), channel_id=1, replica_groups=mesh['ctx_0'=16,'ctx_1'=4,'tp'=8] {'ctx_0'}, dimensions={0}, use_global_device_ids=true | all-gather | bytes 557056 | tf_op jit(solution)/shard_map/all_gather | solution.py:18
  118.8 25.7 %all_gather.35 = bf16[2048,1,128]{2,0,1:T(8,128)(2,1)} all-gather(bf16[128,1,128]{2,0,1:T(8,128)(2,1)S(1)} %all_gather.34), channel_id=1, replica_groups=mesh['ctx_0'=16,'ctx_1'=4,'tp'=8] {'ctx_0'}, dimensions={0}, use_global_device_ids=true | all-gather | bytes 557056 | tf_op jit(solution)/shard_map/all_gather | solution.py:18
  144.6 23.5 %all_gather.39 = bf16[2048,1,128]{2,0,1:T(8,128)(2,1)S(1)} all-gather(bf16[128,1,128]{2,0,1:T(8,128)(2,1)S(1)} %all_gather.38), channel_id=1, replica_groups=mesh['ctx_0'=16,'ctx_1'=4,'tp'=8] {'ctx_0'}, dimensions={0}, use_global_device_ids=true | all-gather | bytes 557056 | tf_op jit(solution)/shard_map/all_gather | solution.py:18
  168.1 42.7 %all-to-all-start.4 = ((bf16[2,4,64,128]{3,1,0,2:T(4,128)(2,1)}), bf16[2,4,64,128]{3,1,0,2:T(4,128)(2,1)S(1)}, u32[]{:S(2)}, u32[]{:S(2)}) async-start(bf16[2,4,64,128]{3,1,0,2:T(4,128)(2,1)} %copy.54), calls=%async_computation.4 | async-start | bytes 262144 | tf_op jit(solution)/shard_map/all_to_all | solution.py:135
  211.5 4.6 conditional.4
  221.7 8.2 %conditional.7 = (f32[1,64,32,1,128]{4,2,1,3,0:T(8,128)S(1)}, f32[1,64,32,1,128]{4,2,1,3,0:T(8,128)S(1)}, bf16[1,32,8,128]{3,2,0,1:T(8,128)(2,1)S(1)}) conditional(s32[]{:T(128)} %convert_element_type.128, () %tuple.70, (s32[32]{0:T(128)S(1)}, bf16[2048,1,128]{2,0,1:T(8,128)(2,1)S(1)}, bf16[32,1,8,128]{3,0,2,1:T(8,128)(2,1)S(1)}, ...), branch_computations={%region_12.0_spmd, %region_13.15_spmd} | conditional | flops 2687991808 | bytes 22157576 | solution.py:127
  230.6 10.5 %conditional.6 = (f32[1,64,32,1,128]{4,2,1,3,0:T(8,128)S(1)}, f32[1,64,32,1,128]{4,2,1,3,0:T(8,128)S(1)}, bf16[1,32,8,128]{3,2,0,1:T(8,128)(2,1)S(1)}) conditional(s32[]{:T(128)} %convert_element_type.128, () %tuple.68, (s32[32]{0:T(128)}, bf16[2048,1,128]{2,0,1:T(8,128)(2,1)S(1)}, bf16[32,1,8,128]{3,0,2,1:T(8,128)(2,1)}, f32[32,1,8]{0,2,1:T(8,128)}, ...), branch_computations={%region_9.10_spmd, %region_10.0_spmd} | conditional | flops 2687991808 | bytes 17438872 | solution.py:127
  251.1 4.5 pad_maximum_fusion
  255.6 280.0 %all-reduce.2 = bf16[64,16384]{1,0:T(8,128)(2,1)S(1)} all-reduce(f32[64,16384]{1,0:T(8,128)} %pad_maximum_fusion), channel_id=2, replica_groups=mesh['ctx_0'=16,'ctx_1'=4,'tp'=8] {'ctx_0','ctx_1'}, use_global_device_ids=true, to_apply=%region_15.16.clone | all-reduce | flops 1048576 | bytes 6291456
  537.2 57.4 %all-to-all-start.6 = ((bf16[2,32,1,128]{3,0,2,1:T(2,128)(2,1)}), bf16[2,32,1,128]{3,0,2,1:T(2,128)(2,1)S(1)}, u32[]{:S(2)}, u32[]{:S(2)}) async-start(bf16[2,32,1,128]{3,0,2,1:T(2,128)(2,1)} %copy.65), calls=%async_computation.6 | async-start | bytes 32768 | tf_op jit(solution)/shard_map/all_to_all | solution.py:211
  599.3 4.0 all-to-all-start.7
  603.9 4.0 all-to-all-done.7
  607.9 4.0 all-to-all-start.3
  612.6 4.6 all-to-all-done.3
  617.2 4.1 all-to-all-start.5
  (112 shorter events, 63.7 us)
Async XLA Ops:
  2.0 17.4 %all-to-all-start = ((bf16[2,4,8,128]{3,1,0,2:T(4,128)(2,1)}), bf16[2,4,8,128]{3,1,0,2:T(4,128)(2,1)S(1)}, u32[]{:S(2)}, u32[]{:S(2)}) async-start(bf16[2,4,8,128]{3,1,0,2:T(4,128)(2,1)} %copy.44), calls=%async_computation | async-start | bytes 32768 | tf_op jit(solution)/shard_map/all_to_all | solution.py:133
  12.0 209.7 %copy-start.15 = (s32[32]{0:T(128)}, s32[32]{0:T(128)S(1)}, u32[]{:S(2)}) copy-start(s32[32]{0:T(128)S(1)} %iota_add_fusion) | copy-start | bytes 388
  19.3 9.5 %all-to-all-start.2 = ((bf16[2,4,8,128]{3,1,0,2:T(4,128)(2,1)}), bf16[2,4,8,128]{3,1,0,2:T(4,128)(2,1)S(1)}, u32[]{:S(2)}, u32[]{:S(2)}) async-start(bf16[2,4,8,128]{3,1,0,2:T(4,128)(2,1)} %copy.47), calls=%async_computation.2 | async-start | bytes 32768 | tf_op jit(solution)/shard_map/all_to_all | solution.py:134
  28.8 139.3 %all-to-all-start.1 = ((bf16[2,4,64,128]{3,1,0,2:T(4,128)(2,1)}), bf16[2,4,64,128]{3,1,0,2:T(4,128)(2,1)S(1)}, u32[]{:S(2)}, u32[]{:S(2)}) async-start(bf16[2,4,64,128]{3,1,0,2:T(4,128)(2,1)} %copy.45), calls=%async_computation.1 | async-start | bytes 262144 | tf_op jit(solution)/shard_map/all_to_all | solution.py:132
  168.1 53.5 %all-to-all-start.4 = ((bf16[2,4,64,128]{3,1,0,2:T(4,128)(2,1)}), bf16[2,4,64,128]{3,1,0,2:T(4,128)(2,1)S(1)}, u32[]{:S(2)}, u32[]{:S(2)}) async-start(bf16[2,4,64,128]{3,1,0,2:T(4,128)(2,1)} %copy.54), calls=%async_computation.4 | async-start | bytes 262144 | tf_op jit(solution)/shard_map/all_to_all | solution.py:135
  216.1 0.6 copy-start.11
  216.1 0.6 copy-start.13
  220.3 0.6 copy-start.12
  220.3 0.6 copy-start.14
  221.9 2.1 copy-start.2
  221.9 2.1 copy-start.4
  224.7 1.8 copy-start.3
  227.0 1.1 copy-start.5
  229.9 0.6 copy-start.7
  241.1 1.0 copy-start
  241.1 1.3 copy-start.1
  241.1 4.8 copy-start.9
  255.6 347.7 %copy-start.6 = (bf16[1,32,8,128]{3,2,0,1:T(8,128)(2,1)S(1)}, bf16[1,32,8,128]{3,2,0,1:T(8,128)(2,1)}, u32[]{:S(2)}) copy-start(bf16[1,32,8,128]{3,2,0,1:T(8,128)(2,1)} %fusion.100) | copy-start | bytes 196612
  255.6 356.3 %copy-start.8 = (bf16[1,32,8,128]{3,2,0,1:T(8,128)(2,1)S(1)}, bf16[1,32,8,128]{3,2,0,1:T(8,128)(2,1)}, u32[]{:S(2)}) copy-start(bf16[1,32,8,128]{3,2,0,1:T(8,128)(2,1)} %copy-done.7) | copy-start | bytes 196612
  255.6 356.3 %copy-start.10 = (bf16[1,32,8,128]{3,2,0,1:T(8,128)(2,1)S(1)}, bf16[1,32,8,128]{3,2,0,1:T(8,128)(2,1)}, u32[]{:S(2)}) copy-start(bf16[1,32,8,128]{3,2,0,1:T(8,128)(2,1)} %copy-done.9) | copy-start | bytes 196612
  537.2 62.1 %all-to-all-start.6 = ((bf16[2,32,1,128]{3,0,2,1:T(2,128)(2,1)}), bf16[2,32,1,128]{3,0,2,1:T(2,128)(2,1)S(1)}, u32[]{:S(2)}, u32[]{:S(2)}) async-start(bf16[2,32,1,128]{3,0,2,1:T(2,128)(2,1)} %copy.65), calls=%async_computation.6 | async-start | bytes 32768 | tf_op jit(solution)/shard_map/all_to_all | solution.py:211
  599.3 8.6 %all-to-all-start.7 = ((bf16[2,32,1,128]{3,0,2,1:T(2,128)(2,1)}), bf16[2,32,1,128]{3,0,2,1:T(2,128)(2,1)S(1)}, u32[]{:S(2)}, u32[]{:S(2)}) async-start(bf16[2,32,1,128]{3,0,2,1:T(2,128)(2,1)} %copy.67), calls=%async_computation.7 | async-start | bytes 32768 | tf_op jit(solution)/shard_map/all_to_all | solution.py:212
  607.9 9.3 %all-to-all-start.3 = ((bf16[2,32,8,128]{3,2,0,1:T(8,128)(2,1)}), bf16[2,32,8,128]{3,2,0,1:T(8,128)(2,1)S(1)}, u32[]{:S(2)}, u32[]{:S(2)}) async-start(bf16[2,32,8,128]{3,2,0,1:T(8,128)(2,1)} %pad_maximum_fusion.1), calls=%async_computation.3 | async-start | bytes 262144 | tf_op jit(solution)/shard_map/all_to_all | solution.py:205
  617.2 9.4 %all-to-all-start.5 = ((bf16[2,32,8,128]{3,2,0,1:T(8,128)(2,1)}), bf16[2,32,8,128]{3,2,0,1:T(8,128)(2,1)S(1)}, u32[]{:S(2)}, u32[]{:S(2)}) async-start(bf16[2,32,8,128]{3,2,0,1:T(8,128)(2,1)} %pad_maximum_fusion.2), calls=%async_computation.5 | async-start | bytes 262144 | tf_op jit(solution)/shard_map/all_to_all | solution.py:208
where the time goes:
time: 629 us; the launch traced here: 627 us
  blocking collectives  415 us (66%)
  starting transfers between devices  131 us (21%)
  local copies, waits for them, and re-layouts  21.6 us (3%)
  waiting for transfers between devices  20.5 us (3%)
  matrix products  20.1 us (3%)
  other arithmetic  16.5 us (3%)
    unnamed x1, blocking collectives  280 us
    all_gather x8, blocking collectives, gather_axes(): value = lax.all_gather(value, axis, axis=dim, tiled=True)  135 us
    all_to_all x1, starting transfers between devices, on_device(): lax.all_to_all(key_sum.astype(jnp.bfloat16), 'tp', split_axis=1, concat_a...  57.4 us
    all_to_all x1, starting transfers between devices, on_device(): lax.all_to_all(result_cotangent, 'tp', split_axis=2, concat_axis=1, tiled...  42.7 us
  transfers between devices with their start and end apart: 8, of which 5 were waited for; matrix products, arithmetic and copies ran while one was open for 3% of the time, Pallas kernels for 0%

commit v1 on v0

v1 whole, which is shorter than its diff:
```python
import functools

import jax
import jax.numpy as jnp
from jax import lax
from jax.experimental import pallas as pl
from jax.experimental.pallas import tpu as pltpu
from jax.sharding import Mesh
from jax.sharding import PartitionSpec as P

MESH = pl.DeviceIdType.MESH
F32 = jnp.float32
BF16 = jnp.bfloat16
NZ, NY, NX = 16, 4, 4
MASKED = -1e30


def nt(a, b):
    return lax.dot_general(a, b, (((1,), (1,)), ((), ())), preferred_element_type=F32)


def nn(a, b):
    return lax.dot_general(a, b, (((1,), (0,)), ((), ())), preferred_element_type=F32)


def split(a):
    high = a.astype(BF16)
    return high, (a - high.astype(F32)).astype(BF16)


def kernel(
    q_hbm, g_hbm, kv_hbm, o_hbm, dq_hbm, dkv_ref,
    q_home, g_home, kv_home, q_rows, g_rows, kv_all,
    keys, values, keys_t, values_t, diagonal, scores, probs, dscores, g_twice, q_twice,
    o_rows, dq_rows, part, other, arrived, final,
    in_sem, zkv_s, zkv_r, zq_s, zq_r, zg_s, zg_r, ag_s, ag_r, fw_s, fw_r,
    o_s, o_r, dq_s, dq_r, sib_s, sib_r, rs_s, rs_r, fin_s, fin_r,
):
    z, y, x, c = (lax.axis_index(a) for a in ("z", "y", "x", "c"))
    chip = y * NX + x
    layer, group = z // 8, lax.rem(z, 8)
    scale = 128 ** -0.5

    stage = [
        pltpu.make_async_copy(kv_hbm, kv_home, in_sem.at[0]),
        pltpu.make_async_copy(kv_hbm.at[layer, group], kv_all.at[chip, c, z], in_sem.at[1]),
        pltpu.make_async_copy(q_hbm, q_home, in_sem.at[2]),
        pltpu.make_async_copy(g_hbm, g_home, in_sem.at[3]),
        pltpu.make_async_copy(q_hbm.at[layer, :, group], q_rows.at[z], in_sem.at[4]),
        pltpu.make_async_copy(g_hbm.at[layer, :, group], g_rows.at[z], in_sem.at[5]),
    ]
    for copy in stage:
        copy.start()

    def z_at(d):
        return lax.rem(z + d, NZ)

    def chip_at(e, sign):
        dy, dx = e // NX, lax.rem(e, NX)
        return lax.rem(y + NY + sign * dy, NY), lax.rem(x + NX + sign * dx, NX)

    barrier = pltpu.get_barrier_semaphore()

    def greet(d, _):
        pl.semaphore_signal(barrier, inc=1, device_id=(z_at(d), y, x, c), device_id_type=MESH)
        pl.semaphore_signal(barrier, inc=1, device_id=(z_at(d), y, x, 1 - c), device_id_type=MESH)
        yy, xx = chip_at(d, 1)
        pl.semaphore_signal(barrier, inc=1, device_id=(z, yy, xx, c), device_id_type=MESH)
        return 0

    lax.fori_loop(1, 16, greet, 0)
    pl.semaphore_signal(barrier, inc=1, device_id=(z, y, x, 1 - c), device_id_type=MESH)

    key_row = lax.broadcasted_iota(jnp.int32, (512, 128), 0)
    lane = lax.broadcasted_iota(jnp.int32, (512, 128), 1)
    key_pos = 128 * ((key_row // 8) % 4) + 8 * (key_row // 32) + key_row % 8
    row_pos = 128 * (lane // 32) + (lane // 8) % 4 + 8 * chip + 4 * c
    diagonal[...] = key_pos - row_pos
    identity = (
        lax.broadcasted_iota(jnp.int32, (128, 128), 0)
        == lax.broadcasted_iota(jnp.int32, (128, 128), 1)
    ).astype(F32).astype(BF16)

    for copy in stage:
        copy.wait()
    pl.semaphore_wait(barrier, 46)

    def to_z(src, dst, send, recv):
        def make(d):
            t = z_at(d)
            return pltpu.make_async_remote_copy(
                src_ref=src(t // 8, lax.rem(t, 8)), dst_ref=dst, send_sem=send.at[d],
                recv_sem=recv.at[d], device_id=(t, y, x, c), device_id_type=MESH,
            )
        return make

    zkv = to_z(lambda l, g: kv_home.at[l, g], kv_all.at[chip, c, z], zkv_s, zkv_r)
    zq = to_z(lambda l, g: q_home.at[l, :, g], q_rows.at[z], zq_s, zq_r)
    zg = to_z(lambda l, g: g_home.at[l, :, g], g_rows.at[z], zg_s, zg_r)

    def loop(low, high, body):
        def step(i, _):
            body(i)
            return 0
        lax.fori_loop(low, high, step, 0)

    loop(1, 16, lambda d: zkv(d).start())
    loop(1, 16, lambda d: zq(d).start())
    loop(1, 16, lambda d: zg(d).start())
    loop(1, 16, lambda d: zkv(d).wait_recv())

    def gather(e):
        yy, xx = chip_at(e, 1)
        return pltpu.make_async_remote_copy(
            src_ref=kv_all.at[chip, c], dst_ref=kv_all.at[chip, c], send_sem=ag_s.at[e],
            recv_sem=ag_r.at[e], device_id=(z, yy, xx, c), device_id_type=MESH,
        )

    def forward(e):
        yy, xx = chip_at(e, -1)
        block = kv_all.at[yy * NX + xx, c]
        return pltpu.make_async_remote_copy(
            src_ref=block, dst_ref=block, send_sem=fw_s.at[e],
            recv_sem=fw_r.at[e], device_id=(z, y, x, 1 - c), device_id_type=MESH,
        )

    loop(1, 16, lambda e: gather(e).start())
    forward(0).start()

    def pass_on(e):
        gather(e).wait_recv()
        forward(e).start()

    loop(1, 16, pass_on)

    low_half = lax.rem(lax.broadcasted_iota(jnp.int32, (128, 128), 0), 8) < 4

    def unpack(e):
        forward(e).wait_recv()
        yy, xx = chip_at(e, -1)
        j = yy * NX + xx
        a = kv_all[j, 0].astype(F32).reshape(128, 128)
        b = kv_all[j, 1].astype(F32).reshape(128, 128)
        k = jnp.where(low_half, a, pltpu.roll(b, 4, 0)).astype(BF16)
        v = jnp.where(low_half, pltpu.roll(a, 124, 0), b).astype(BF16)
        at = pl.ds(pl.multiple_of(j * 32, 32), 32)
        for kg in range(4):
            keys[kg, at, :] = k[32 * kg : 32 * kg + 32]
            values[kg, at, :] = v[32 * kg : 32 * kg + 32]

    loop(0, 16, unpack)

    def transposed(kg):
        keys_t[kg] = nt(identity, keys[kg]).astype(BF16)
        values_t[kg] = nt(identity, values[kg]).astype(BF16)

    loop(0, 4, transposed)
    loop(1, 16, lambda d: zq(d).wait_recv())
    loop(1, 16, lambda d: zg(d).wait_recv())

    def home(rows, out, send, recv):
        def make(t, s):
            return pltpu.make_async_remote_copy(
                src_ref=rows.at[t], dst_ref=out.at[layer, :, group], send_sem=send.at[t],
                recv_sem=recv.at[s], device_id=(t, y, x, c), device_id_type=MESH,
            )
        def own():
            return pltpu.make_async_copy(rows.at[z], out.at[layer, :, group], recv.at[z])
        def start(t):
            @pl.when(t != z)
            def _():
                make(t, z).start()
            @pl.when(t == z)
            def _():
                own().start()
        def finish(t):
            @pl.when(t != z)
            def _():
                make(t, t).wait_recv()
                make(t, z).wait_send()
            @pl.when(t == z)
            def _():
                own().wait()
        return start, finish

    o_start, o_finish = home(o_rows, o_hbm, o_s, o_r)
    dq_start, dq_finish = home(dq_rows, dq_hbm, dq_s, dq_r)

    for rg in range(4):
        q = q_rows[4 * rg : 4 * rg + 4].astype(F32).reshape(128, 128).astype(BF16)
        g = g_rows[4 * rg : 4 * rg + 4].astype(F32).reshape(128, 128).astype(BF16)
        for twice, value in ((q_twice, q), (g_twice, g)):
            twice[256 * rg : 256 * rg + 128] = value
            twice[256 * rg + 128 : 256 * rg + 256] = value
        g_t = nt(identity, g)

        def score(kg, top, last):
            s = nt(keys[kg], q) * scale
            if last:
                s = jnp.where(diagonal[...] <= 0, s, MASKED)
            scores[kg] = s
            return jnp.maximum(top, jnp.max(s.reshape(64, 8, 128), axis=0))

        top = jnp.full((8, 128), MASKED, F32)
        top = lax.fori_loop(0, rg, lambda kg, t: score(kg, t, False), top)
        top = score(rg, top, True)
        top = jnp.max(top, axis=0, keepdims=True)

        def attend(kg, carry):
            total, acc = carry
            p = jnp.exp(scores[kg] - top)
            total = total + jnp.sum(p.reshape(64, 8, 128), axis=0)
            acc = acc + nn(values_t[kg], jnp.concatenate(split(p), axis=1))
            return total, acc

        total, acc = lax.fori_loop(
            0, rg + 1, attend, (jnp.zeros((8, 128), F32), jnp.zeros((128, 256), F32))
        )
        total = jnp.sum(total, axis=0, keepdims=True)
        o_t = (acc[:, :128] + acc[:, 128:]) / total
        log_norm = top + jnp.log(total)
        row_delta = jnp.sum(g_t * o_t.astype(BF16).astype(F32), axis=0, keepdims=True)
        o_rows[4 * rg : 4 * rg + 4] = o_t.T.reshape(4, 4, 8, 128).astype(BF16)
        loop(4 * rg, 4 * rg + 4, o_start)

        def backward(kg, acc):
            p = jnp.exp(scores[kg] - log_norm)
            ds = p * (nt(values[kg], g) - row_delta)
            p2 = jnp.concatenate(split(p), axis=1)
            ds2 = jnp.concatenate(split(ds), axis=1)
            probs[kg, :, 256 * rg : 256 * rg + 256] = p2
            dscores[kg, :, 256 * rg : 256 * rg + 256] = ds2
            return acc + nn(keys_t[kg], ds2)

        acc = lax.fori_loop(0, rg + 1, backward, jnp.zeros((128, 256), F32))
        dq_t = (acc[:, :128] + acc[:, 128:]) * scale
        dq_rows[4 * rg : 4 * rg + 4] = dq_t.T.reshape(4, 4, 8, 128).astype(BF16)
        loop(4 * rg, 4 * rg + 4, dq_start)

    def sibling(kg):
        return pltpu.make_async_remote_copy(
            src_ref=part.at[1 - c, kg], dst_ref=other.at[kg], send_sem=sib_s.at[kg],
            recv_sem=sib_r.at[kg], device_id=(z, y, x, 1 - c), device_id_type=MESH,
        )

    def scatter(kg, e):
        yy, xx = chip_at(e, 1)
        rows = pl.ds(pl.multiple_of((yy * NX + xx) * 32, 32), 32)
        return pltpu.make_async_remote_copy(
            src_ref=part.at[c, kg, rows], dst_ref=arrived.at[e, kg], send_sem=rs_s.at[kg, e],
            recv_sem=rs_r.at[kg, e], device_id=(z, yy, xx, c), device_id_type=MESH,
        )

    for kg in range(4):
        part[0, kg] = nn(dscores[kg, :, 256 * kg :], q_twice[256 * kg :])
        part[1, kg] = nn(probs[kg, :, 256 * kg :], g_twice[256 * kg :])
        sibling(kg).start()

    def combine(kg):
        sibling(kg).wait_recv()
        part[c, kg] = part[c, kg] + other[kg]
        loop(1, 16, lambda e: scatter(kg, e).start())

    loop(0, 4, combine)

    factor = jnp.where(c == 0, scale, 1.0).astype(F32)
    own_rows = pl.ds(pl.multiple_of(chip * 32, 32), 32)

    def finish(kg):
        loop(1, 16, lambda e: scatter(kg, e).wait_recv())
        total = lax.fori_loop(
            1, 16, lambda e, t: t + arrived[e, kg], part[c, kg, own_rows]
        ) * factor
        final[pl.ds(4 * kg, 4)] = total.reshape(4, 8, 128).astype(BF16)

    loop(0, 4, finish)

    def out(d, core):
        t = z_at(d)
        return pltpu.make_async_remote_copy(
            src_ref=final.at[t], dst_ref=dkv_ref.at[c, z], send_sem=fin_s.at[d, core],
            recv_sem=fin_r.at[d, c], device_id=(t, y, x, core), device_id_type=MESH,
        )

    def into(d, core):
        t = z_at(d)
        return pltpu.make_async_remote_copy(
            src_ref=final.at[t], dst_ref=dkv_ref.at[c, z], send_sem=fin_s.at[d, core],
            recv_sem=fin_r.at[d, core], device_id=(t, y, x, c), device_id_type=MESH,
        )

    dkv_ref[c, z] = final[z]
    out(0, 1 - c).start()
    loop(1, 16, lambda d: (out(d, c).start(), out(d, 1 - c).start()))

    loop(1, 16, lambda d: (zkv(d).wait_send(), zq(d).wait_send(), zg(d).wait_send()))
    loop(1, 16, lambda e: gather(e).wait_send())
    loop(0, 16, lambda e: forward(e).wait_send())
    loop(0, 16, lambda t: (o_finish(t), dq_finish(t)))
    loop(0, 4, lambda kg: sibling(kg).wait_send())
    loop(0, 4, lambda kg: loop(1, 16, lambda e: scatter(kg, e).wait_send()))
    out(0, 1 - c).wait_send()
    into(0, 1 - c).wait_recv()
    loop(1, 16, lambda d: (out(d, c).wait_send(), out(d, 1 - c).wait_send()))
    loop(1, 16, lambda d: (into(d, c).wait_recv(), into(d, 1 - c).wait_recv()))


def on_device(q, k, v, g):
    core = lax.axis_index("c")
    kv = jnp.concatenate([k.transpose(0, 2, 1, 3), v.transpose(0, 2, 1, 3)], axis=2)
    wide = (2, 4, 8, 8, 128)
    dma = pltpu.SemaphoreType.DMA
    hbm = pl.BlockSpec(memory_space=pltpu.MemorySpace.HBM)
    vmem = pl.BlockSpec(memory_space=pltpu.VMEM)
    o, dq, dkv = pl.pallas_call(
        kernel,
        out_shape=(
            jax.ShapeDtypeStruct(wide, BF16),
            jax.ShapeDtypeStruct(wide, BF16),
            jax.ShapeDtypeStruct((2, 16, 8, 128), BF16),
        ),
        in_specs=[hbm, hbm, hbm],
        out_specs=(hbm, hbm, vmem),
        scratch_shapes=[
            pltpu.VMEM(wide, BF16),
            pltpu.VMEM(wide, BF16),
            pltpu.VMEM((2, 8, 8, 128), BF16),
            pltpu.VMEM((16, 4, 8, 128), BF16),
            pltpu.VMEM((16, 4, 8, 128), BF16),
            pltpu.VMEM((16, 2, 16, 8, 128), BF16),
            pltpu.VMEM((4, 512, 128), BF16),
            pltpu.VMEM((4, 512, 128), BF16),
            pltpu.VMEM((4, 128, 512), BF16),
            pltpu.VMEM((4, 128, 512), BF16),
            pltpu.VMEM((512, 128), jnp.int32),
            pltpu.VMEM((4, 512, 128), F32),
            pltpu.VMEM((4, 512, 1024), BF16),
            pltpu.VMEM((4, 512, 1024), BF16),
            pltpu.VMEM((1024, 128), BF16),
            pltpu.VMEM((1024, 128), BF16),
            pltpu.VMEM((16, 4, 8, 128), BF16),
            pltpu.VMEM((16, 4, 8, 128), BF16),
            pltpu.VMEM((2, 4, 512, 128), F32),
            pltpu.VMEM((4, 512, 128), F32),
            pltpu.VMEM((16, 4, 32, 128), F32),
            pltpu.VMEM((16, 8, 128), BF16),
            dma((6,)),
            dma((16,)), dma((16,)), dma((16,)), dma((16,)), dma((16,)), dma((16,)),
            dma((16,)), dma((16,)), dma((16,)), dma((16,)),
            dma((16,)), dma((16,)), dma((16,)), dma((16,)),
            dma((4,)), dma((4,)), dma((4, 16)), dma((4, 16)), dma((16, 2)), dma((16, 2)),
        ],
        compiler_params=pltpu.CompilerParams(
            collective_id=1, has_side_effects=True, vmem_limit_bytes=48 * 2**20
        ),
        name="attend",
    )(q.reshape(wide), g.reshape(wide), kv)
    dkv = lax.dynamic_slice_in_dim(dkv.reshape(2, 2, 8, 8, 128), 4 * core, 4, 3)
    dkv = dkv.transpose(0, 1, 3, 2, 4)
    return o.reshape(q.shape), dq.reshape(q.shape), dkv[0], dkv[1]


def solution(mesh):
    grid = Mesh(mesh.devices.reshape(NZ, NY, NX, 2), ("z", "y", "x", "c"))
    spec = P(None, ("z", "y", "x", "c"), None, None)
    return jax.shard_map(
        on_device, mesh=grid, in_specs=(spec,) * 4, out_specs=(spec,) * 4, check_vma=False
    )
```

time: 629 us -> 81.8 us (0.13)
  blocking collectives: 415 us -> 0 us
  starting transfers between devices: 131 us -> 0 us
  Pallas kernels: 0 us -> 76.2 us
  waiting for transfers between devices: 20.5 us -> 0 us
  matrix products: 20.1 us -> 0 us
  local copies, waits for them, and re-layouts: 21.6 us -> 3.75 us
  other arithmetic: 16.5 us -> 0.02 us
    unnamed x1 -> x0, blocking collectives: 280 us -> none
    all_gather x8 -> x0, blocking collectives: 135 us -> none  [gather_axes(): value = lax.all_gather(value, axis, axis=dim, tiled=True)]
    all_to_all x8 -> x0, starting transfers between devices: 131 us -> none  [the longest x1 57.4 us: on_device(): lax.all_to_all(key_sum.astype(jnp.bfloat16), 'tp', split_axis=1, concat_a...]
    pallas_call x0 -> x1, Pallas kernels: none -> 76.2 us  [on_device(): pl.pallas_call(kernel, out_shape=(jax.ShapeDtypeStruct(wide, BF16), jax.S...]
    all_to_all x8 -> x0, waiting for transfers between devices: 20.5 us -> none  [the longest x1 4.64 us: on_device(): lax.all_to_all(content_vectors, 'tp', split_axis=2, concat_axis=1, tiled=...]
    dot_general x14 -> x0, matrix products: 20.1 us -> none  [the longest x2 4.49 us: update(): jnp.einsum('tkgn,tkgd->nkd', dscore, expanded_asking_vectors, precision=l...]
    unnamed x31 -> x7, local copies, waits for them, and re-layouts: 11.5 us -> 2.33 us
  transfers between devices with their start and end apart: 8 -> 0, of which waited for: 5 -> 0; matrix products, arithmetic and copies ran while one was open for 3% -> 0% of each run, Pallas kernels for 0% -> 0%
where the time goes in v1:
time: 81.8 us; the launch traced here: 80.6 us
  Pallas kernels  76.2 us (93%)
  local copies, waits for them, and re-layouts  3.75 us (5%)
    pallas_call x1, Pallas kernels, on_device(): pl.pallas_call(kernel, out_shape=(jax.ShapeDtypeStruct(wide, BF16), jax.S...  76.2 us
    unnamed x7, local copies, waits for them, and re-layouts  2.33 us

profile of v1, /device:TPU:1, one launch (start us, length us, event | category | flops | bytes accessed | tf_op | source)
XLA Modules:
  0.0 80.6 jit_solution(9595409452606393860)
XLA Ops:
  0.6 0.0 copy-start
  0.6 0.8 copy_bitcast_fusion.1
  1.5 0.1 copy-done
  1.6 0.0 copy-start.1
  1.6 0.9 %copy-done.1 = bf16[2,4,64,128]{3,2,1,0:T(8,128)(2,1)S(1)} copy-done((bf16[2,4,64,128]{3,2,1,0:T(8,128)(2,1)S(1)}, bf16[2,4,64,128]{3,2,1,0:T(8,128)(2,1)}, u32[]{:S(2)}) %copy-start.1) | copy-done | bytes 131096
  2.5 76.2 %attend.1 = (bf16[2,4,8,8,128]{4,3,2,1,0:T(8,128)(2,1)S(1)}, bf16[2,4,8,8,128]{4,3,2,1,0:T(8,128)(2,1)S(1)}, bf16[2,16,8,128]{3,2,1,0:T(8,128)(2,1)S(1)}) custom-call(bf16[2,4,8,8,128]{4,3,2,1,0:T(8,128)(2,1)S(1)} %bitcast.16, bf16[2,4,8,8,128]{4,3,2,1,0:T(8,128)(2,1)S(1)} %bitcast.17, bf16[2,8,8,128]{3,2,1,0:T(8,128)(2,1)S(1)} %pad_maximum_fusion.kv_hbm), custom_call_target="tpu_custom_call" | custom-call | tf_op jit(solution)/shard_map/attend/pallas_call | solution.py:315
  78.7 0.6 slice_bitcast_fusion
  79.3 0.7 copy.18
  80.0 0.7 copy.19
  (3 shorter events, 0.1 us)
Async XLA Ops:
  0.6 0.9 %copy-start = (bf16[2,4,64,128]{3,2,1,0:T(8,128)(2,1)S(1)}, bf16[2,4,64,128]{3,2,1,0:T(8,128)(2,1)}, u32[]{:S(2)}) copy-start(bf16[2,4,64,128]{3,2,1,0:T(8,128)(2,1)} %param.4) | copy-start | bytes 393220
  1.6 0.9 %copy-start.1 = (bf16[2,4,64,128]{3,2,1,0:T(8,128)(2,1)S(1)}, bf16[2,4,64,128]{3,2,1,0:T(8,128)(2,1)}, u32[]{:S(2)}) copy-start(bf16[2,4,64,128]{3,2,1,0:T(8,128)(2,1)} %param.7) | copy-start | bytes 393220

commit v2 on v1

v2 whole, which is shorter than its diff:
```python
import functools

import jax
import jax.numpy as jnp
from jax import lax
from jax.experimental import pallas as pl
from jax.experimental.pallas import tpu as pltpu
from jax.sharding import Mesh
from jax.sharding import PartitionSpec as P

MESH = pl.DeviceIdType.MESH
F32 = jnp.float32
BF16 = jnp.bfloat16
NZ, NY, NX = 16, 4, 4
MASKED = -1e30


def nt(a, b):
    return lax.dot_general(a, b, (((1,), (1,)), ((), ())), preferred_element_type=F32)


def nn(a, b):
    return lax.dot_general(a, b, (((1,), (0,)), ((), ())), preferred_element_type=F32)


def split(a):
    high = a.astype(BF16)
    return high, (a - high.astype(F32)).astype(BF16)


def kernel(
    q_hbm, k_hbm, v_hbm, g_hbm, o_hbm, dq_hbm, dkv_ref,
    q_home, k_home, v_home, g_home, kv_wide, kv_home, q_rows, g_rows, kv_all,
    keys, values, keys_t, values_t, diagonal, scores, probs, dscores, g_twice, q_twice,
    o_rows, dq_rows, part, other, arrived, final,
    in_sem, zkv_s, zkv_r, zq_s, zq_r, zg_s, zg_r, ag_s, ag_r, fw_s, fw_r,
    o_s, o_r, dq_s, dq_r, sib_s, sib_r, rs_s, rs_r, fin_s, fin_r,
):
    z, y, x, c = (lax.axis_index(a) for a in ("z", "y", "x", "c"))
    chip = y * NX + x
    layer, group = z // 8, lax.rem(z, 8)
    scale = 128 ** -0.5

    stage = [
        pltpu.make_async_copy(k_hbm, k_home, in_sem.at[0]),
        pltpu.make_async_copy(v_hbm, v_home, in_sem.at[1]),
        pltpu.make_async_copy(q_hbm, q_home, in_sem.at[2]),
        pltpu.make_async_copy(g_hbm, g_home, in_sem.at[3]),
        pltpu.make_async_copy(q_hbm.at[layer, :, group], q_rows.at[z], in_sem.at[4]),
        pltpu.make_async_copy(g_hbm.at[layer, :, group], g_rows.at[z], in_sem.at[5]),
    ]
    for copy in stage:
        copy.start()

    def z_at(d):
        return lax.rem(z + d, NZ)

    def chip_at(e, sign):
        dy, dx = e // NX, lax.rem(e, NX)
        return lax.rem(y + NY + sign * dy, NY), lax.rem(x + NX + sign * dx, NX)

    barrier = pltpu.get_barrier_semaphore()

    def greet(d, _):
        pl.semaphore_signal(barrier, inc=1, device_id=(z_at(d), y, x, c), device_id_type=MESH)
        pl.semaphore_signal(barrier, inc=1, device_id=(z_at(d), y, x, 1 - c), device_id_type=MESH)
        yy, xx = chip_at(d, 1)
        pl.semaphore_signal(barrier, inc=1, device_id=(z, yy, xx, c), device_id_type=MESH)
        return 0

    lax.fori_loop(1, 16, greet, 0)
    pl.semaphore_signal(barrier, inc=1, device_id=(z, y, x, 1 - c), device_id_type=MESH)

    key_row = lax.broadcasted_iota(jnp.int32, (512, 128), 0)
    lane = lax.broadcasted_iota(jnp.int32, (512, 128), 1)
    key_pos = 128 * ((key_row >> 3) & 3) + 8 * (key_row >> 5) + (key_row & 7)
    row_pos = 128 * (lane >> 5) + ((lane >> 3) & 3) + 8 * chip + 4 * c
    diagonal[...] = key_pos - row_pos
    identity = (
        lax.broadcasted_iota(jnp.int32, (128, 128), 0)
        == lax.broadcasted_iota(jnp.int32, (128, 128), 1)
    ).astype(F32).astype(BF16)

    with jax.named_scope("p0_kv"):
        stage[0].wait()
        stage[1].wait()
        for l in range(2):
            for i in range(4):
                kv_wide[l, :, i, :] = k_home[l, i].astype(F32)
                kv_wide[l, :, 4 + i, :] = v_home[l, i].astype(F32)
        kv_home[...] = kv_wide[...].astype(BF16)
        kv_all[chip, c, 8] = kv_wide[layer, group].astype(BF16)
        for copy in stage[2:]:
            copy.wait()
    with jax.named_scope("p1_barrier"):
        pl.semaphore_wait(barrier, 46)

    def to_z(src, dst, send, recv):
        def make(d):
            t = z_at(d)
            return pltpu.make_async_remote_copy(
                src_ref=src(t // 8, lax.rem(t, 8)), dst_ref=dst(d), send_sem=send.at[d],
                recv_sem=recv.at[d], device_id=(t, y, x, c), device_id_type=MESH,
            )
        return make

    zkv = to_z(
        lambda l, g: kv_home.at[l, g], lambda d: kv_all.at[chip, c, (24 - d) & 15], zkv_s, zkv_r
    )
    zq = to_z(lambda l, g: q_home.at[l, :, g], lambda d: q_rows.at[z], zq_s, zq_r)
    zg = to_z(lambda l, g: g_home.at[l, :, g], lambda d: g_rows.at[z], zg_s, zg_r)

    def loop(low, high, body):
        def step(i, _):
            body(i)
            return 0
        lax.fori_loop(low, high, step, 0)

    with jax.named_scope("p2_zstart"):
        loop(1, 16, lambda d: zkv(d).start())
        loop(1, 16, lambda d: zq(d).start())
        loop(1, 16, lambda d: zg(d).start())
    PIECES = ((4, 9), (0, 4), (13, 3))

    def gather(n, e):
        yy, xx = chip_at(e, 1)
        block = kv_all.at[chip, c, pl.ds(*PIECES[n])]
        return pltpu.make_async_remote_copy(
            src_ref=block, dst_ref=block, send_sem=ag_s.at[n, e],
            recv_sem=ag_r.at[n, e], device_id=(z, yy, xx, c), device_id_type=MESH,
        )

    def forward(n, e):
        yy, xx = chip_at(e, -1)
        block = kv_all.at[yy * NX + xx, c, pl.ds(*PIECES[n])]
        return pltpu.make_async_remote_copy(
            src_ref=block, dst_ref=block, send_sem=fw_s.at[n, e],
            recv_sem=fw_r.at[n, e], device_id=(z, y, x, 1 - c), device_id_type=MESH,
        )

    with jax.named_scope("p3_zkv"):
        loop(1, 5, lambda d: zkv(d).wait_recv())
        loop(12, 16, lambda d: zkv(d).wait_recv())
        loop(1, 16, lambda e: gather(0, e).start())
        forward(0, 0).start()
        loop(5, 12, lambda d: zkv(d).wait_recv())
        for n in (1, 2):
            loop(1, 16, lambda e: gather(n, e).start())
            forward(n, 0).start()

    low_half = lax.broadcasted_iota(jnp.int32, (8, 128), 0) < 4

    def pass_on(n, e):
        gather(n, e).wait_recv()
        forward(n, e).start()

    def unpack(e):
        for n in range(3):
            forward(n, e).wait_recv()
        yy, xx = chip_at(e, -1)
        j = yy * NX + xx
        ks, vs = [], []
        for plane in range(16):
            slot = (plane + 24 - z) & 15
            a = kv_all[j, 0, slot].astype(F32)
            b = kv_all[j, 1, slot].astype(F32)
            ks.append(jnp.where(low_half, a, pltpu.roll(b, 4, 0)))
            vs.append(jnp.where(low_half, pltpu.roll(a, 4, 0), b))
        at = pl.ds(pl.multiple_of(j * 32, 32), 32)
        for kg in range(4):
            keys[kg, at, :] = jnp.concatenate(ks[4 * kg : 4 * kg + 4], axis=0).astype(BF16)
            values[kg, at, :] = jnp.concatenate(vs[4 * kg : 4 * kg + 4], axis=0).astype(BF16)

    with jax.named_scope("p5_agwait"):
        loop(1, 16, lambda e: pass_on(0, e))

        def last(e):
            pass_on(1, e)
            pass_on(2, e)

        def step(e):
            last(e)
            unpack(e - 2)

        loop(1, 2, last)
        loop(2, 16, step)
    with jax.named_scope("p6_unpack"):
        loop(14, 16, unpack)

    with jax.named_scope("p8_qwait"):
        loop(1, 16, lambda d: zq(d).wait_recv())
        loop(1, 16, lambda d: zg(d).wait_recv())

    def home(rows, out, send, recv):
        def make(t, s):
            return pltpu.make_async_remote_copy(
                src_ref=rows.at[t], dst_ref=out.at[layer, :, group], send_sem=send.at[t],
                recv_sem=recv.at[s], device_id=(t, y, x, c), device_id_type=MESH,
            )
        def own():
            return pltpu.make_async_copy(rows.at[z], out.at[layer, :, group], recv.at[z])
        def start(t):
            @pl.when(t != z)
            def _():
                make(t, z).start()
            @pl.when(t == z)
            def _():
                own().start()
        def finish(t):
            @pl.when(t != z)
            def _():
                make(t, t).wait_recv()
                make(t, z).wait_send()
            @pl.when(t == z)
            def _():
                own().wait()
        return start, finish

    o_start, o_finish = home(o_rows, o_hbm, o_s, o_r)
    dq_start, dq_finish = home(dq_rows, dq_hbm, dq_s, dq_r)

    factor_2 = scale * 1.4426950408889634

    def block_of(rg):
        q = q_rows[4 * rg : 4 * rg + 4].astype(F32).reshape(128, 128).astype(BF16)
        g = g_rows[4 * rg : 4 * rg + 4].astype(F32).reshape(128, 128).astype(BF16)
        for twice, value in ((q_twice, q), (g_twice, g)):
            twice[256 * rg : 256 * rg + 128] = value
            twice[256 * rg + 128 : 256 * rg + 256] = value
        lanes = slice(256 * rg, 256 * rg + 256)
        top = jnp.full((8, 128), MASKED, F32)
        for kg in range(rg + 1):
            s = nt(keys[kg], q) * factor_2
            if kg == rg:
                s = jnp.where(diagonal[...] <= 0, s, MASKED)
            scores[rg % 2, kg] = s
            top = jnp.maximum(top, jnp.max(s.reshape(64, 8, 128), axis=0))
        top = jnp.max(top, axis=0, keepdims=True)
        total = jnp.zeros((8, 128), F32)
        for kg in range(rg + 1):
            e = jnp.exp2(scores[rg % 2, kg] - top)
            scores[rg % 2, kg] = e
            total = total + jnp.sum(e.reshape(64, 8, 128), axis=0)
        inverse = 1.0 / jnp.sum(total, axis=0, keepdims=True)
        acc = jnp.zeros((128, 256), F32)
        for kg in range(rg + 1):
            p = scores[rg % 2, kg] * inverse
            p2 = jnp.concatenate(split(p), axis=1)
            probs[kg, :, lanes] = p2
            scores[rg % 2, kg] = p
            acc = acc + nn(values_t[kg], p2)
        o_t = acc[:, :128] + acc[:, 128:]
        row_delta = jnp.sum(nt(identity, g) * o_t.astype(BF16).astype(F32), axis=0, keepdims=True)
        o_rows[4 * rg : 4 * rg + 4] = o_t.T.reshape(4, 4, 8, 128).astype(BF16)
        acc = jnp.zeros((128, 256), F32)
        for kg in range(rg + 1):
            ds = scores[rg % 2, kg] * (nt(values[kg], g) - row_delta)
            ds2 = jnp.concatenate(split(ds), axis=1)
            dscores[kg, :, lanes] = ds2
            acc = acc + nn(keys_t[kg], ds2)
        dq_t = (acc[:, :128] + acc[:, 128:]) * scale
        dq_rows[4 * rg : 4 * rg + 4] = dq_t.T.reshape(4, 4, 8, 128).astype(BF16)

    with jax.named_scope("p9_rg01"):
        for kg in range(4):
            keys_t[kg] = nt(identity, keys[kg]).astype(BF16)
            values_t[kg] = nt(identity, values[kg]).astype(BF16)
        block_of(0)
        block_of(1)
    loop(0, 8, lambda t: (o_start(t), dq_start(t)))
    with jax.named_scope("p9_rg23"):
        block_of(2)
        block_of(3)
    loop(8, 16, lambda t: (o_start(t), dq_start(t)))

    def sibling(kg):
        return pltpu.make_async_remote_copy(
            src_ref=part.at[1 - c, kg], dst_ref=other.at[kg], send_sem=sib_s.at[kg],
            recv_sem=sib_r.at[kg], device_id=(z, y, x, 1 - c), device_id_type=MESH,
        )

    def scatter(kg, e):
        yy, xx = chip_at(e, 1)
        rows = pl.ds(pl.multiple_of((yy * NX + xx) * 32, 32), 32)
        return pltpu.make_async_remote_copy(
            src_ref=part.at[c, kg, rows], dst_ref=arrived.at[e, kg], send_sem=rs_s.at[kg, e],
            recv_sem=rs_r.at[kg, e], device_id=(z, yy, xx, c), device_id_type=MESH,
        )

    with jax.named_scope("pa_dkv"):
        for kg in range(4):
            part[0, kg] = nn(dscores[kg, :, 256 * kg :], q_twice[256 * kg :])
            part[1, kg] = nn(probs[kg, :, 256 * kg :], g_twice[256 * kg :])
            sibling(kg).start()

    def combine(kg):
        sibling(kg).wait_recv()
        part[c, kg] = part[c, kg] + other[kg]
        loop(1, 16, lambda e: scatter(kg, e).start())

    with jax.named_scope("pb_combine"):
        loop(0, 4, combine)

    factor = jnp.where(c == 0, scale, 1.0).astype(F32)
    own_rows = pl.ds(pl.multiple_of(chip * 32, 32), 32)

    def finish(kg):
        loop(1, 16, lambda e: scatter(kg, e).wait_recv())
        total = lax.fori_loop(
            1, 16, lambda e, t: t + arrived[e, kg], part[c, kg, own_rows]
        ) * factor
        final[pl.ds(4 * kg, 4)] = total.reshape(4, 8, 128).astype(BF16)

    with jax.named_scope("pc_rs"):
        loop(0, 4, finish)

    def out(d, core):
        t = z_at(d)
        return pltpu.make_async_remote_copy(
            src_ref=final.at[t], dst_ref=dkv_ref.at[c, z], send_sem=fin_s.at[d, core],
            recv_sem=fin_r.at[d, c], device_id=(t, y, x, core), device_id_type=MESH,
        )

    def into(d, core):
        t = z_at(d)
        return pltpu.make_async_remote_copy(
            src_ref=final.at[t], dst_ref=dkv_ref.at[c, z], send_sem=fin_s.at[d, core],
            recv_sem=fin_r.at[d, core], device_id=(t, y, x, c), device_id_type=MESH,
        )

    with jax.named_scope("pd_start"):
        dkv_ref[c, z] = final[z]
        out(0, 1 - c).start()
        loop(1, 16, lambda d: (out(d, c).start(), out(d, 1 - c).start()))

    with jax.named_scope("pe_sends"):
        loop(1, 16, lambda d: (zkv(d).wait_send(), zq(d).wait_send(), zg(d).wait_send()))
        for n in range(3):
            loop(1, 16, lambda e: gather(n, e).wait_send())
            loop(0, 16, lambda e: forward(n, e).wait_send())
        loop(0, 16, lambda t: (o_finish(t), dq_finish(t)))
        loop(0, 4, lambda kg: sibling(kg).wait_send())
        loop(0, 4, lambda kg: loop(1, 16, lambda e: scatter(kg, e).wait_send()))
    with jax.named_scope("pf_dkv"):
        out(0, 1 - c).wait_send()
        into(0, 1 - c).wait_recv()
        loop(1, 16, lambda d: (out(d, c).wait_send(), out(d, 1 - c).wait_send()))
        loop(1, 16, lambda d: (into(d, c).wait_recv(), into(d, 1 - c).wait_recv()))


def on_device(q, k, v, g):
    core = lax.axis_index("c")
    wide = (2, 4, 8, 8, 128)
    dma = pltpu.SemaphoreType.DMA
    hbm = pl.BlockSpec(memory_space=pltpu.MemorySpace.HBM)
    vmem = pl.BlockSpec(memory_space=pltpu.VMEM)
    o, dq, dkv = pl.pallas_call(
        kernel,
        out_shape=(
            jax.ShapeDtypeStruct(wide, BF16),
            jax.ShapeDtypeStruct(wide, BF16),
            jax.ShapeDtypeStruct((2, 16, 8, 128), BF16),
        ),
        in_specs=[hbm, hbm, hbm, hbm],
        out_specs=(hbm, hbm, vmem),
        scratch_shapes=[
            pltpu.VMEM(wide, BF16),
            pltpu.VMEM((2, 4, 8, 128), BF16),
            pltpu.VMEM((2, 4, 8, 128), BF16),
            pltpu.VMEM(wide, BF16),
            pltpu.VMEM((2, 8, 8, 128), F32),
            pltpu.VMEM((2, 8, 8, 128), BF16),
            pltpu.VMEM((16, 4, 8, 128), BF16),
            pltpu.VMEM((16, 4, 8, 128), BF16),
            pltpu.VMEM((16, 2, 16, 8, 128), BF16),
            pltpu.VMEM((4, 512, 128), BF16),
            pltpu.VMEM((4, 512, 128), BF16),
            pltpu.VMEM((4, 128, 512), BF16),
            pltpu.VMEM((4, 128, 512), BF16),
            pltpu.VMEM((512, 128), jnp.int32),
            pltpu.VMEM((2, 4, 512, 128), F32),
            pltpu.VMEM((4, 512, 1024), BF16),
            pltpu.VMEM((4, 512, 1024), BF16),
            pltpu.VMEM((1024, 128), BF16),
            pltpu.VMEM((1024, 128), BF16),
            pltpu.VMEM((16, 4, 8, 128), BF16),
            pltpu.VMEM((16, 4, 8, 128), BF16),
            pltpu.VMEM((2, 4, 512, 128), F32),
            pltpu.VMEM((4, 512, 128), F32),
            pltpu.VMEM((16, 4, 32, 128), F32),
            pltpu.VMEM((16, 8, 128), BF16),
            dma((6,)),
            dma((16,)), dma((16,)), dma((16,)), dma((16,)), dma((16,)), dma((16,)),
            dma((3, 16)), dma((3, 16)), dma((3, 16)), dma((3, 16)),
            dma((16,)), dma((16,)), dma((16,)), dma((16,)),
            dma((4,)), dma((4,)), dma((4, 16)), dma((4, 16)), dma((16, 2)), dma((16, 2)),
        ],
        compiler_params=pltpu.CompilerParams(
            collective_id=1, has_side_effects=True, vmem_limit_bytes=67043328
        ),
        name="attend",
    )(q.reshape(wide), k, v, g.reshape(wide))
    dkv = lax.dynamic_slice_in_dim(dkv.reshape(2, 2, 8, 8, 128), 4 * core, 4, 3)
    dkv = dkv.transpose(0, 1, 3, 2, 4)
    return o.reshape(q.shape), dq.reshape(q.shape), dkv[0], dkv[1]


def solution(mesh):
    grid = Mesh(mesh.devices.reshape(NZ, NY, NX, 2), ("z", "y", "x", "c"))
    spec = P(None, ("z", "y", "x", "c"), None, None)
    return jax.shard_map(
        on_device, mesh=grid, in_specs=(spec,) * 4, out_specs=(spec,) * 4, check_vma=False
    )
```

time: 81.8 us -> 78.4 us (0.958)
  Pallas kernels: 76.2 us -> 73.4 us
    pallas_call x1, Pallas kernels: 76.2 us -> 73.4 us  [on_device(): pl.pallas_call(kernel, out_shape=(jax.ShapeDtypeStruct(wide, BF16), jax.S...]
    dynamic_slice x1, local copies, waits for them, and re-layouts: 0.03 us -> 0.9 us  [on_device(): dkv = lax.dynamic_slice_in_dim(dkv.reshape(2, 2, 8, 8, 128), 4 * core, 4, 3)]
where the time goes in v2:
time: 78.4 us; the launch traced here: 77.2 us
  Pallas kernels  73.4 us (94%)
  local copies, waits for them, and re-layouts  3.13 us (4%)
    pallas_call x1, Pallas kernels, on_device(): pl.pallas_call(kernel, out_shape=(jax.ShapeDtypeStruct(wide, BF16), jax.S...  73.4 us
    unnamed x7, local copies, waits for them, and re-layouts  1.62 us

profile of v2, /device:TPU:1, one launch (start us, length us, event | category | flops | bytes accessed | tf_op | source)
XLA Modules:
  0.0 77.2 jit_solution(9791008564901138910)
XLA Ops:
  0.6 73.4 %attend.1 = (bf16[2,4,8,8,128]{4,3,2,1,0:T(8,128)(2,1)}, bf16[2,4,8,8,128]{4,3,2,1,0:T(8,128)(2,1)}, bf16[2,16,8,128]{3,2,1,0:T(8,128)(2,1)}) custom-call(bf16[2,4,8,8,128]{4,3,2,1,0:T(8,128)(2,1)} %bitcast.12, bf16[2,4,8,128]{3,2,1,0:T(8,128)(2,1)} %k_hbm.1, bf16[2,4,8,128]{3,2,1,0:T(8,128)(2,1)} %v_hbm.1, bf16[2,4,8,8,128]{4,3,2,1,0:T(8,128)(2,1)} %bitcast.13), custom_call_target="tpu_custom_call" | custom-call | tf_op jit(solution)/shard_map/attend/pallas_call | solution.py:357
  74.1 0.0 copy-start.1
  74.1 0.9 %constant_dynamic-slice_fusion = bf16[2,2,8,4,128]{4,3,2,1,0:T(4,128)(2,1)S(1)} fusion(bf16[2,2,8,8,128]{4,3,2,1,0:T(8,128)(2,1)} %bitcast.17, s32[]{:T(128)S(6)} %select_n.3), kind=kLoop, calls=%fused_computation.3 | loop fusion | bytes 65540 | tf_op jit(solution)/shard_map/dynamic_slice | solution.py:403
  75.0 0.6 slice_bitcast_fusion
  75.6 0.0 copy-done.1
  75.6 0.0 copy-start
  75.6 0.7 copy.14
  76.3 0.3 copy-done
  76.6 0.7 copy.15
  (1 shorter events, 0.0 us)
Async XLA Ops:
  74.1 1.5 %copy-start.1 = (bf16[2,4,8,8,128]{4,3,2,1,0:T(8,128)(2,1)S(1)}, bf16[2,4,8,8,128]{4,3,2,1,0:T(8,128)(2,1)}, u32[]{:S(2)}) copy-start(bf16[2,4,8,8,128]{4,3,2,1,0:T(8,128)(2,1)} %get-tuple-element.7) | copy-start | bytes 393220
  75.6 1.0 %copy-start = (bf16[2,4,8,8,128]{4,3,2,1,0:T(8,128)(2,1)S(1)}, bf16[2,4,8,8,128]{4,3,2,1,0:T(8,128)(2,1)}, u32[]{:S(2)}) copy-start(bf16[2,4,8,8,128]{4,3,2,1,0:T(8,128)(2,1)} %get-tuple-element.8) | copy-start | bytes 393220

commit v3 on v2

--- a/solution.py
+++ b/solution.py
@@ -31,10 +31,10 @@
 def kernel(
     q_hbm, k_hbm, v_hbm, g_hbm, o_hbm, dq_hbm, dkv_ref,
     q_home, k_home, v_home, g_home, kv_wide, kv_home, q_rows, g_rows, kv_all,
-    keys, values, keys_t, values_t, diagonal, scores, probs, dscores, g_twice, q_twice,
-    o_rows, dq_rows, part, other, arrived, final,
+    mate, keys_t, values_t, diagonal, scores, probs, dscores, g_twice, q_twice,
+    o_rows, dq_rows, part, other, row_in, row_sum, block_in, final,
     in_sem, zkv_s, zkv_r, zq_s, zq_r, zg_s, zg_r, ag_s, ag_r, fw_s, fw_r,
-    o_s, o_r, dq_s, dq_r, sib_s, sib_r, rs_s, rs_r, fin_s, fin_r,
+    o_s, o_r, dq_s, dq_r, sib_s, sib_r, row_s, row_r, blk_s, blk_r, fin_s, fin_r,
 ):
     z, y, x, c = (lax.axis_index(a) for a in ("z", "y", "x", "c"))
     chip = y * NX + x
@@ -71,9 +71,8 @@
     lax.fori_loop(1, 16, greet, 0)
     pl.semaphore_signal(barrier, inc=1, device_id=(z, y, x, 1 - c), device_id_type=MESH)
 
-    key_row = lax.broadcasted_iota(jnp.int32, (512, 128), 0)
+    key_pos = lax.broadcasted_iota(jnp.int32, (512, 128), 0)
     lane = lax.broadcasted_iota(jnp.int32, (512, 128), 1)
-    key_pos = 128 * ((key_row >> 3) & 3) + 8 * (key_row >> 5) + (key_row & 7)
     row_pos = 128 * (lane >> 5) + ((lane >> 3) & 3) + 8 * chip + 4 * c
     diagonal[...] = key_pos - row_pos
     identity = (
@@ -89,7 +88,6 @@
                 kv_wide[l, :, i, :] = k_home[l, i].astype(F32)
                 kv_wide[l, :, 4 + i, :] = v_home[l, i].astype(F32)
         kv_home[...] = kv_wide[...].astype(BF16)
-        kv_all[chip, c, 8] = kv_wide[layer, group].astype(BF16)
         for copy in stage[2:]:
             copy.wait()
     with jax.named_scope("p1_barrier"):
@@ -99,16 +97,36 @@
         def make(d):
             t = z_at(d)
             return pltpu.make_async_remote_copy(
-                src_ref=src(t // 8, lax.rem(t, 8)), dst_ref=dst(d), send_sem=send.at[d],
+                src_ref=src.at[t // 8, :, lax.rem(t, 8)], dst_ref=dst.at[z], send_sem=send.at[d],
                 recv_sem=recv.at[d], device_id=(t, y, x, c), device_id_type=MESH,
             )
         return make
 
-    zkv = to_z(
-        lambda l, g: kv_home.at[l, g], lambda d: kv_all.at[chip, c, (24 - d) & 15], zkv_s, zkv_r
+    half = pl.ds(pl.multiple_of(4 * c, 4), 4)
+
+    def to_core(core, d):
+        t = z_at(d)
+        return pltpu.make_async_remote_copy(
+            src_ref=kv_home.at[t // 8, lax.rem(t, 8), pl.ds(4 * core, 4)],
+            dst_ref=kv_all.at[core, (24 - d) & 15, chip, half],
+            send_sem=zkv_s.at[core, d], recv_sem=zkv_r.at[c, d],
+            device_id=(t, y, x, core), device_id_type=MESH,
+        )
+
+    def from_core(core, d):
+        return pltpu.make_async_remote_copy(
+            src_ref=kv_home.at[0, 0, pl.ds(0, 4)],
+            dst_ref=kv_all.at[c, (24 - d) & 15, chip, pl.ds(4 * core, 4)],
+            send_sem=zkv_s.at[core, d], recv_sem=zkv_r.at[core, d],
+            device_id=(z_at(d), y, x, core), device_id_type=MESH,
+        )
+
+    own_kv = pltpu.make_async_remote_copy(
+        src_ref=kv_home.at[layer, group], dst_ref=mate, send_sem=zkv_s.at[0, 0],
+        recv_sem=zkv_r.at[0, 0], device_id=(z, y, x, 1 - c), device_id_type=MESH,
     )
-    zq = to_z(lambda l, g: q_home.at[l, :, g], lambda d: q_rows.at[z], zq_s, zq_r)
-    zg = to_z(lambda l, g: g_home.at[l, :, g], lambda d: g_rows.at[z], zg_s, zg_r)
+    zq = to_z(q_home, q_rows, zq_s, zq_r)
+    zg = to_z(g_home, g_rows, zg_s, zg_r)
 
     def loop(low, high, body):
         def step(i, _):
@@ -117,14 +135,16 @@
         lax.fori_loop(low, high, step, 0)
 
     with jax.named_scope("p2_zstart"):
-        loop(1, 16, lambda d: zkv(d).start())
+        own_kv.start()
+        loop(1, 16, lambda d: (to_core(0, d).start(), to_core(1, d).start()))
         loop(1, 16, lambda d: zq(d).start())
         loop(1, 16, lambda d: zg(d).start())
+
     PIECES = ((4, 9), (0, 4), (13, 3))
 
     def gather(n, e):
         yy, xx = chip_at(e, 1)
-        block = kv_all.at[chip, c, pl.ds(*PIECES[n])]
+        block = kv_all.at[c, pl.ds(*PIECES[n]), chip]
         return pltpu.make_async_remote_copy(
             src_ref=block, dst_ref=block, send_sem=ag_s.at[n, e],
             recv_sem=ag_r.at[n, e], device_id=(z, yy, xx, c), device_id_type=MESH,
@@ -132,60 +152,56 @@
 
     def forward(n, e):
         yy, xx = chip_at(e, -1)
-        block = kv_all.at[yy * NX + xx, c, pl.ds(*PIECES[n])]
+        block = kv_all.at[c, pl.ds(*PIECES[n]), yy * NX + xx]
         return pltpu.make_async_remote_copy(
             src_ref=block, dst_ref=block, send_sem=fw_s.at[n, e],
             recv_sem=fw_r.at[n, e], device_id=(z, y, x, 1 - c), device_id_type=MESH,
         )
 
-    with jax.named_scope("p3_zkv"):
-        loop(1, 5, lambda d: zkv(d).wait_recv())
-        loop(12, 16, lambda d: zkv(d).wait_recv())
+    def backward(n, e):
+        yy, xx = chip_at(e, -1)
+        block = kv_all.at[1 - c, pl.ds(*PIECES[n]), yy * NX + xx]
+        return pltpu.make_async_remote_copy(
+            src_ref=block, dst_ref=block, send_sem=fw_s.at[n, e],
+            recv_sem=fw_r.at[n, e], device_id=(z, y, x, 1 - c), device_id_type=MESH,
+        )
+
+    def received(d):
+        from_core(0, d).wait_recv()
+        from_core(1, d).wait_recv()
+
+    with jax.named_scope("p3_zkvn"):
+        own_kv.wait_recv()
+        mine = kv_wide[layer, group]
+        theirs = pltpu.roll(mate[...].astype(F32), 4, 0)
+        low_half = (lax.broadcasted_iota(jnp.int32, (8, 128), 0) >> 2) == c
+        kv_all[c, 8, chip] = jnp.where(low_half, mine, theirs).astype(BF16)
+        loop(1, 5, received)
+        loop(12, 16, received)
         loop(1, 16, lambda e: gather(0, e).start())
         forward(0, 0).start()
-        loop(5, 12, lambda d: zkv(d).wait_recv())
+    with jax.named_scope("p3_zkvf"):
+        loop(5, 12, received)
         for n in (1, 2):
             loop(1, 16, lambda e: gather(n, e).start())
             forward(n, 0).start()
 
-    low_half = lax.broadcasted_iota(jnp.int32, (8, 128), 0) < 4
-
     def pass_on(n, e):
         gather(n, e).wait_recv()
         forward(n, e).start()
 
-    def unpack(e):
+    with jax.named_scope("p4_agnear"):
+        loop(1, 16, lambda e: pass_on(0, e))
+    with jax.named_scope("p5_agfar"):
+        loop(1, 16, lambda e: (pass_on(1, e), pass_on(2, e)))
+    with jax.named_scope("p6_fwd"):
         for n in range(3):
-            forward(n, e).wait_recv()
-        yy, xx = chip_at(e, -1)
-        j = yy * NX + xx
-        ks, vs = [], []
-        for plane in range(16):
-            slot = (plane + 24 - z) & 15
-            a = kv_all[j, 0, slot].astype(F32)
-            b = kv_all[j, 1, slot].astype(F32)
-            ks.append(jnp.where(low_half, a, pltpu.roll(b, 4, 0)))
-            vs.append(jnp.where(low_half, pltpu.roll(a, 4, 0), b))
-        at = pl.ds(pl.multiple_of(j * 32, 32), 32)
-        for kg in range(4):
-            keys[kg, at, :] = jnp.concatenate(ks[4 * kg : 4 * kg + 4], axis=0).astype(BF16)
-            values[kg, at, :] = jnp.concatenate(vs[4 * kg : 4 * kg + 4], axis=0).astype(BF16)
-
-    with jax.named_scope("p5_agwait"):
-        loop(1, 16, lambda e: pass_on(0, e))
-
-        def last(e):
-            pass_on(1, e)
-            pass_on(2, e)
-
-        def step(e):
-            last(e)
-            unpack(e - 2)
-
-        loop(1, 2, last)
-        loop(2, 16, step)
-    with jax.named_scope("p6_unpack"):
-        loop(14, 16, unpack)
+            loop(0, 16, lambda e: backward(n, e).wait_recv())
+
+    def plane_group(kind, kg):
+        return jnp.concatenate(
+            [kv_all[kind, (4 * kg + i + 24 - z) & 15].reshape(128, 128) for i in range(4)], axis=0
+        )
 
     with jax.named_scope("p8_qwait"):
         loop(1, 16, lambda d: zq(d).wait_recv())
@@ -230,7 +246,7 @@
         lanes = slice(256 * rg, 256 * rg + 256)
         top = jnp.full((8, 128), MASKED, F32)
         for kg in range(rg + 1):
-            s = nt(keys[kg], q) * factor_2
+            s = nt(plane_group(0, kg), q) * factor_2
             if kg == rg:
                 s = jnp.where(diagonal[...] <= 0, s, MASKED)
             scores[rg % 2, kg] = s
@@ -254,7 +270,7 @@
         o_rows[4 * rg : 4 * rg + 4] = o_t.T.reshape(4, 4, 8, 128).astype(BF16)
         acc = jnp.zeros((128, 256), F32)
         for kg in range(rg + 1):
-            ds = scores[rg % 2, kg] * (nt(values[kg], g) - row_delta)
+            ds = scores[rg % 2, kg] * (nt(plane_group(1, kg), g) - row_delta)
             ds2 = jnp.concatenate(split(ds), axis=1)
             dscores[kg, :, lanes] = ds2
             acc = acc + nn(keys_t[kg], ds2)
@@ -263,8 +279,8 @@
 
     with jax.named_scope("p9_rg01"):
         for kg in range(4):
-            keys_t[kg] = nt(identity, keys[kg]).astype(BF16)
-            values_t[kg] = nt(identity, values[kg]).astype(BF16)
+            keys_t[kg] = nt(identity, plane_group(0, kg)).astype(BF16)
+            values_t[kg] = nt(identity, plane_group(1, kg)).astype(BF16)
         block_of(0)
         block_of(1)
     loop(0, 8, lambda t: (o_start(t), dq_start(t)))
@@ -273,45 +289,69 @@
         block_of(3)
     loop(8, 16, lambda t: (o_start(t), dq_start(t)))
 
+    along = jnp.where(c == 0, x, y)
+    across = jnp.where(c == 0, y, x)
+
     def sibling(kg):
         return pltpu.make_async_remote_copy(
             src_ref=part.at[1 - c, kg], dst_ref=other.at[kg], send_sem=sib_s.at[kg],
             recv_sem=sib_r.at[kg], device_id=(z, y, x, 1 - c), device_id_type=MESH,
         )
 
-    def scatter(kg, e):
-        yy, xx = chip_at(e, 1)
-        rows = pl.ds(pl.multiple_of((yy * NX + xx) * 32, 32), 32)
-        return pltpu.make_async_remote_copy(
-            src_ref=part.at[c, kg, rows], dst_ref=arrived.at[e, kg], send_sem=rs_s.at[kg, e],
-            recv_sem=rs_r.at[kg, e], device_id=(z, yy, xx, c), device_id_type=MESH,
-        )
-
-    with jax.named_scope("pa_dkv"):
-        for kg in range(4):
-            part[0, kg] = nn(dscores[kg, :, 256 * kg :], q_twice[256 * kg :])
-            part[1, kg] = nn(probs[kg, :, 256 * kg :], g_twice[256 * kg :])
-            sibling(kg).start()
+    def row_send(kg, a):
+        t = (along + a) & 3
+        return pltpu.make_async_remote_copy(
+            src_ref=part.at[c, kg, :, t], dst_ref=row_in.at[a, kg], send_sem=row_s.at[kg, a],
+            recv_sem=row_r.at[kg, a],
+            device_id=(z, jnp.where(c == 0, y, t), jnp.where(c == 0, t, x), c), device_id_type=MESH,
+        )
+
+    def block_send(kg, a):
+        t = (across + a) & 3
+        return pltpu.make_async_remote_copy(
+            src_ref=row_sum.at[kg, :, t], dst_ref=block_in.at[a, kg], send_sem=blk_s.at[kg, a],
+            recv_sem=blk_r.at[kg, a],
+            device_id=(z, jnp.where(c == 0, t, y), jnp.where(c == 0, x, t), c), device_id_type=MESH,
+        )
 
     def combine(kg):
         sibling(kg).wait_recv()
         part[c, kg] = part[c, kg] + other[kg]
-        loop(1, 16, lambda e: scatter(kg, e).start())
+        loop(1, 4, lambda a: row_send(kg, a).start())
+
+    with jax.named_scope("pa_dkv"):
+        for kg in range(4):
+            dk = nn(dscores[kg, :, 256 * kg :], q_twice[256 * kg :])
+            dv = nn(probs[kg, :, 256 * kg :], g_twice[256 * kg :])
+            part[0, kg] = jnp.swapaxes(dk.reshape(4, 4, 4, 8, 128), 1, 2)
+            part[1, kg] = dv.reshape(4, 4, 4, 8, 128)
+            sibling(kg).start()
+            if kg:
+                combine(kg - 1)
 
     with jax.named_scope("pb_combine"):
-        loop(0, 4, combine)
+        combine(3)
+
+    def row_finish(kg):
+        total = part[c, kg, :, along]
+        for a in range(1, 4):
+            row_send(kg, a).wait_recv()
+            total = total + row_in[a, kg]
+        row_sum[kg] = total
+        loop(1, 4, lambda a: block_send(kg, a).start())
 
     factor = jnp.where(c == 0, scale, 1.0).astype(F32)
-    own_rows = pl.ds(pl.multiple_of(chip * 32, 32), 32)
 
     def finish(kg):
-        loop(1, 16, lambda e: scatter(kg, e).wait_recv())
-        total = lax.fori_loop(
-            1, 16, lambda e, t: t + arrived[e, kg], part[c, kg, own_rows]
-        ) * factor
-        final[pl.ds(4 * kg, 4)] = total.reshape(4, 8, 128).astype(BF16)
-
-    with jax.named_scope("pc_rs"):
+        total = row_sum[kg, :, across]
+        for a in range(1, 4):
+            block_send(kg, a).wait_recv()
+            total = total + block_in[a, kg]
+        final[pl.ds(4 * kg, 4)] = (total * factor).astype(BF16)
+
+    with jax.named_scope("pc_rows"):
+        loop(0, 4, row_finish)
+    with jax.named_scope("pc_blocks"):
         loop(0, 4, finish)
 
     def out(d, core):
@@ -334,13 +374,15 @@
         loop(1, 16, lambda d: (out(d, c).start(), out(d, 1 - c).start()))
 
     with jax.named_scope("pe_sends"):
-        loop(1, 16, lambda d: (zkv(d).wait_send(), zq(d).wait_send(), zg(d).wait_send()))
+        own_kv.wait_send()
+        loop(1, 16, lambda d: (to_core(0, d).wait_send(), to_core(1, d).wait_send()))
+        loop(1, 16, lambda d: (zq(d).wait_send(), zg(d).wait_send()))
         for n in range(3):
             loop(1, 16, lambda e: gather(n, e).wait_send())
             loop(0, 16, lambda e: forward(n, e).wait_send())
         loop(0, 16, lambda t: (o_finish(t), dq_finish(t)))
         loop(0, 4, lambda kg: sibling(kg).wait_send())
-        loop(0, 4, lambda kg: loop(1, 16, lambda e: scatter(kg, e).wait_send()))
+        loop(0, 4, lambda kg: loop(1, 4, lambda a: (row_send(kg, a).wait_send(), block_send(kg, a).wait_send())))
     with jax.named_scope("pf_dkv"):
         out(0, 1 - c).wait_send()
         into(0, 1 - c).wait_recv()
@@ -372,9 +414,8 @@
             pltpu.VMEM((2, 8, 8, 128), BF16),
             pltpu.VMEM((16, 4, 8, 128), BF16),
             pltpu.VMEM((16, 4, 8, 128), BF16),
-            pltpu.VMEM((16, 2, 16, 8, 128), BF16),
-            pltpu.VMEM((4, 512, 128), BF16),
-            pltpu.VMEM((4, 512, 128), BF16),
+            pltpu.VMEM((2, 16, 16, 8, 128), BF16),
+            pltpu.VMEM((8, 128), BF16),
             pltpu.VMEM((4, 128, 512), BF16),
             pltpu.VMEM((4, 128, 512), BF16),
             pltpu.VMEM((512, 128), jnp.int32),
@@ -385,15 +426,17 @@
             pltpu.VMEM((1024, 128), BF16),
             pltpu.VMEM((16, 4, 8, 128), BF16),
             pltpu.VMEM((16, 4, 8, 128), BF16),
-            pltpu.VMEM((2, 4, 512, 128), F32),
-            pltpu.VMEM((4, 512, 128), F32),
-            pltpu.VMEM((16, 4, 32, 128), F32),
+            pltpu.VMEM((2, 4, 4, 4, 4, 8, 128), F32),
+            pltpu.VMEM((4, 4, 4, 4, 8, 128), F32),
+            pltpu.VMEM((4, 4, 4, 4, 8, 128), F32),
+            pltpu.VMEM((4, 4, 4, 8, 128), F32),
+            pltpu.VMEM((4, 4, 4, 8, 128), F32),
             pltpu.VMEM((16, 8, 128), BF16),
             dma((6,)),
-            dma((16,)), dma((16,)), dma((16,)), dma((16,)), dma((16,)), dma((16,)),
+            dma((2, 16)), dma((2, 16)), dma((16,)), dma((16,)), dma((16,)), dma((16,)),
             dma((3, 16)), dma((3, 16)), dma((3, 16)), dma((3, 16)),
             dma((16,)), dma((16,)), dma((16,)), dma((16,)),
-            dma((4,)), dma((4,)), dma((4, 16)), dma((4, 16)), dma((16, 2)), dma((16, 2)),
+            dma((4,)), dma((4,)), dma((4, 4)), dma((4, 4)), dma((4, 4)), dma((4, 4)), dma((16, 2)), dma((16, 2)),
         ],
         compiler_params=pltpu.CompilerParams(
             collective_id=1, has_side_effects=True, vmem_limit_bytes=67043328

time: 78.4 us -> 77.6 us (0.990); the launches traced: 77.2 us -> 77.4 us
  no operation moved by 1% of the time
where the time goes in v3:
time: 77.6 us; the launch traced here: 77.4 us
  Pallas kernels  73.6 us (95%)
  local copies, waits for them, and re-layouts  3.13 us (4%)
    pallas_call x1, Pallas kernels, on_device(): pl.pallas_call(kernel, out_shape=(jax.ShapeDtypeStruct(wide, BF16), jax.S...  73.6 us
    unnamed x7, local copies, waits for them, and re-layouts  1.62 us

profile of v3, /device:TPU:1, one launch (start us, length us, event | category | flops | bytes accessed | tf_op | source)
XLA Modules:
  0.0 77.4 jit_solution(9870377223434201404)
XLA Ops:
  0.6 73.6 %attend.1 = (bf16[2,4,8,8,128]{4,3,2,1,0:T(8,128)(2,1)}, bf16[2,4,8,8,128]{4,3,2,1,0:T(8,128)(2,1)}, bf16[2,16,8,128]{3,2,1,0:T(8,128)(2,1)}) custom-call(bf16[2,4,8,8,128]{4,3,2,1,0:T(8,128)(2,1)} %bitcast.12, bf16[2,4,8,128]{3,2,1,0:T(8,128)(2,1)} %k_hbm.1, bf16[2,4,8,128]{3,2,1,0:T(8,128)(2,1)} %v_hbm.1, bf16[2,4,8,8,128]{4,3,2,1,0:T(8,128)(2,1)} %bitcast.13), custom_call_target="tpu_custom_call" | custom-call | tf_op jit(solution)/shard_map/attend/pallas_call | solution.py:399
  74.3 0.0 copy-start.1
  74.3 0.9 %constant_dynamic-slice_fusion = bf16[2,2,8,4,128]{4,3,2,1,0:T(4,128)(2,1)S(1)} fusion(bf16[2,2,8,8,128]{4,3,2,1,0:T(8,128)(2,1)} %bitcast.17, s32[]{:T(128)S(6)} %select_n.3), kind=kLoop, calls=%fused_computation.3 | loop fusion | bytes 65540 | tf_op jit(solution)/shard_map/dynamic_slice | solution.py:446
  75.2 0.6 slice_bitcast_fusion
  75.8 0.0 copy-done.1
  75.8 0.0 copy-start
  75.8 0.7 copy.14
  76.5 0.3 copy-done
  76.8 0.7 copy.15
  (1 shorter events, 0.0 us)
Async XLA Ops:
  74.3 1.5 %copy-start.1 = (bf16[2,4,8,8,128]{4,3,2,1,0:T(8,128)(2,1)S(1)}, bf16[2,4,8,8,128]{4,3,2,1,0:T(8,128)(2,1)}, u32[]{:S(2)}) copy-start(bf16[2,4,8,8,128]{4,3,2,1,0:T(8,128)(2,1)} %get-tuple-element.7) | copy-start | bytes 393220
  75.8 1.0 %copy-start = (bf16[2,4,8,8,128]{4,3,2,1,0:T(8,128)(2,1)S(1)}, bf16[2,4,8,8,128]{4,3,2,1,0:T(8,128)(2,1)}, u32[]{:S(2)}) copy-start(bf16[2,4,8,8,128]{4,3,2,1,0:T(8,128)(2,1)} %get-tuple-element.8) | copy-start | bytes 393220

commit v4 on v3

v4 whole, which is shorter than its diff:
```python
import functools

import jax
import jax.numpy as jnp
from jax import lax
from jax.experimental import pallas as pl
from jax.experimental.pallas import tpu as pltpu
from jax.sharding import Mesh
from jax.sharding import PartitionSpec as P

MESH = pl.DeviceIdType.MESH
F32 = jnp.float32
BF16 = jnp.bfloat16
NZ, NY, NX = 16, 4, 4
MASKED = -1e30


def nt(a, b):
    return lax.dot_general(a, b, (((1,), (1,)), ((), ())), preferred_element_type=F32)


def nn(a, b):
    return lax.dot_general(a, b, (((1,), (0,)), ((), ())), preferred_element_type=F32)


def split(a):
    high = a.astype(BF16)
    return high, (a - high.astype(F32)).astype(BF16)


def kernel(
    q_hbm, k_hbm, v_hbm, g_hbm, o_hbm, dq_hbm, dkv_ref,
    q_home, k_home, v_home, g_home, kv_wide, kv_home, q_rows, g_rows, kv_all,
    mate, keys_t, values_t, diagonal, scores, probs, dscores, g_twice, q_twice,
    o_rows, dq_rows, part, other, row_in, row_sum, block_in, final,
    in_sem, zkv_s, zkv_r, own_s, own_r, zq_s, zq_r, zg_s, zg_r, ag_s, ag_r, fw_s, fw_r,
    o_s, o_r, own_o, dq_s, dq_r, own_dq, sib_s, sib_r, row_s, row_r, blk_s, blk_r, fin_s, fin_r,
):
    z, y, x, c = (lax.axis_index(a) for a in ("z", "y", "x", "c"))
    chip = y * NX + x
    layer, group = z >> 3, z & 7
    scale = 128 ** -0.5

    def z_at(d):
        return (z + d) & 15

    def chip_at(e, sign):
        dy, dx = e >> 2, e & 3
        return (y + 4 + sign * dy) & 3, (x + 4 + sign * dx) & 3

    barrier = pltpu.get_barrier_semaphore()

    def greet(*device):
        pl.semaphore_signal(barrier, inc=1, device_id=device, device_id_type=MESH)

    for d in (8, 7, 9, 6, 10, 5, 11, 4, 12, 3, 13, 2, 14, 1, 15):
        greet(z_at(d), y, x, c)
        greet(z_at(d), y, x, 1 - c)
    for e in (10, 6, 9, 11, 14, 2, 8, 5, 7, 13, 15, 1, 3, 4, 12):
        greet(z, *chip_at(e, 1), c)
    greet(z, y, x, 1 - c)

    stage = [
        pltpu.make_async_copy(k_hbm, k_home, in_sem.at[0]),
        pltpu.make_async_copy(v_hbm, v_home, in_sem.at[1]),
        pltpu.make_async_copy(q_hbm, q_home, in_sem.at[2]),
        pltpu.make_async_copy(g_hbm, g_home, in_sem.at[3]),
        pltpu.make_async_copy(q_hbm.at[layer, :, group], q_rows.at[z], in_sem.at[4]),
        pltpu.make_async_copy(g_hbm.at[layer, :, group], g_rows.at[z], in_sem.at[5]),
    ]
    for copy in stage:
        copy.start()

    def drain(ref, sem):
        pltpu.make_async_remote_copy(
            src_ref=ref, dst_ref=ref, send_sem=sem, recv_sem=sem,
            device_id=(z, y, x, 1 - c), device_id_type=MESH,
        ).wait_recv()

    key_pos = lax.broadcasted_iota(jnp.int32, (512, 128), 0)
    lane = lax.broadcasted_iota(jnp.int32, (512, 128), 1)
    row_pos = 128 * (lane >> 5) + ((lane >> 3) & 3) + 8 * chip + 4 * c
    diagonal[...] = key_pos - row_pos
    identity = (
        lax.broadcasted_iota(jnp.int32, (128, 128), 0)
        == lax.broadcasted_iota(jnp.int32, (128, 128), 1)
    ).astype(F32).astype(BF16)

    with jax.named_scope("p0_kv"):
        stage[0].wait()
        stage[1].wait()
        for l in range(2):
            for i in range(4):
                kv_wide[l, :, i, :] = k_home[l, i].astype(F32)
                kv_wide[l, :, 4 + i, :] = v_home[l, i].astype(F32)
        kv_home[...] = kv_wide[...].astype(BF16)
        for copy in stage[2:]:
            copy.wait()
    with jax.named_scope("p1_barrier"):
        pl.semaphore_wait(barrier, 46)

    def to_z(src, dst, send, recv):
        def make(d):
            t = z_at(d)
            return pltpu.make_async_remote_copy(
                src_ref=src.at[t >> 3, :, t & 7], dst_ref=dst.at[z], send_sem=send,
                recv_sem=recv, device_id=(t, y, x, c), device_id_type=MESH,
            )
        return make

    half = pl.ds(pl.multiple_of(4 * c, 4), 4)

    def to_core(core, d, far):
        t = z_at(d)
        return pltpu.make_async_remote_copy(
            src_ref=kv_home.at[t >> 3, t & 7, pl.ds(4 * core, 4)],
            dst_ref=kv_all.at[core, (20 - d) & 15, chip, half],
            send_sem=zkv_s, recv_sem=zkv_r.at[far],
            device_id=(t, y, x, core), device_id_type=MESH,
        )

    own_kv = pltpu.make_async_remote_copy(
        src_ref=kv_home.at[layer, group], dst_ref=mate, send_sem=own_s,
        recv_sem=own_r, device_id=(z, y, x, 1 - c), device_id_type=MESH,
    )
    zq = to_z(q_home, q_rows, zq_s, zq_r)
    zg = to_z(g_home, g_rows, zg_s, zg_r)

    def loop(low, high, body):
        def step(i, _):
            body(i)
            return 0
        lax.fori_loop(low, high, step, 0)

    with jax.named_scope("p2_zstart"):
        own_kv.start()
        def send_kv(d, far):
            to_core(0, d, far).start()
            to_core(1, d, far).start()

        loop(5, 12, lambda d: send_kv(d, 1))
        loop(1, 5, lambda d: send_kv(d, 0))
        loop(12, 16, lambda d: send_kv(d, 0))
        loop(1, 16, lambda d: zq(d).start())
        loop(1, 16, lambda d: zg(d).start())

    PIECES = (pl.ds(0, 9), pl.ds(9, 7))

    def gather(n, e):
        block = kv_all.at[c, PIECES[n], chip]
        return pltpu.make_async_remote_copy(
            src_ref=block, dst_ref=block, send_sem=ag_s,
            recv_sem=ag_r.at[n, e], device_id=(z, *chip_at(e, 1), c), device_id_type=MESH,
        )

    def forward(n, e):
        yy, xx = chip_at(e, -1)
        block = kv_all.at[c, PIECES[n], yy * NX + xx]
        return pltpu.make_async_remote_copy(
            src_ref=block, dst_ref=block, send_sem=fw_s,
            recv_sem=fw_r.at[n], device_id=(z, y, x, 1 - c), device_id_type=MESH,
        )

    with jax.named_scope("p3_zkvn"):
        own_kv.wait_recv()
        mine = kv_wide[layer, group]
        theirs = pltpu.roll(mate[...].astype(F32), 4, 0)
        low_half = (lax.broadcasted_iota(jnp.int32, (8, 128), 0) >> 2) == c
        kv_all[c, 4, chip] = jnp.where(low_half, mine, theirs).astype(BF16)
        drain(kv_home.at[0], zkv_r.at[0])
        loop(1, 16, lambda e: gather(0, e).start())
        forward(0, 0).start()
    with jax.named_scope("p3_zkvf"):
        drain(kv_home.at[0, pl.ds(0, 7)], zkv_r.at[1])
        loop(1, 16, lambda e: gather(1, e).start())
        forward(1, 0).start()

    def pass_on(n, e):
        gather(n, e).wait_recv()
        forward(n, e).start()

    with jax.named_scope("p4_agnear"):
        loop(1, 16, lambda e: pass_on(0, e))
    with jax.named_scope("p5_agfar"):
        loop(1, 16, lambda e: pass_on(1, e))
    with jax.named_scope("p6_fwd"):
        drain(kv_all.at[1 - c, PIECES[0]], fw_r.at[0])
        drain(kv_all.at[1 - c, PIECES[1]], fw_r.at[1])

    def plane_group(kind, kg):
        return jnp.concatenate(
            [kv_all[kind, (4 * kg + i + 20 - z) & 15].reshape(128, 128) for i in range(4)], axis=0
        )

    with jax.named_scope("p8_qwait"):
        drain(q_rows.at[pl.ds(0, 15)], zq_r)
        drain(g_rows.at[pl.ds(0, 15)], zg_r)

    def home(rows, out, send, recv, own_sem):
        def make(t):
            return pltpu.make_async_remote_copy(
                src_ref=rows.at[t], dst_ref=out.at[layer, :, group], send_sem=send,
                recv_sem=recv, device_id=(t, y, x, c), device_id_type=MESH,
            )
        own = pltpu.make_async_copy(rows.at[z], out.at[layer, :, group], own_sem)
        def start(t):
            @pl.when(t != z)
            def _():
                make(t).start()
            @pl.when(t == z)
            def _():
                own.start()
        def finish():
            drain(rows.at[pl.ds(0, 15)], send)
            drain(rows.at[pl.ds(0, 15)], recv)
            own.wait()
        return start, finish

    o_start, o_finish = home(o_rows, o_hbm, o_s, o_r, own_o)
    dq_start, dq_finish = home(dq_rows, dq_hbm, dq_s, dq_r, own_dq)

    factor_2 = scale * 1.4426950408889634

    def block_of(rg):
        q = q_rows[4 * rg : 4 * rg + 4].astype(F32).reshape(128, 128).astype(BF16)
        g = g_rows[4 * rg : 4 * rg + 4].astype(F32).reshape(128, 128).astype(BF16)
        for twice, value in ((q_twice, q), (g_twice, g)):
            twice[256 * rg : 256 * rg + 128] = value
            twice[256 * rg + 128 : 256 * rg + 256] = value
        lanes = slice(256 * rg, 256 * rg + 256)
        top = jnp.full((8, 128), MASKED, F32)
        for kg in range(rg + 1):
            s = nt(plane_group(0, kg), q) * factor_2
            if kg == rg:
                s = jnp.where(diagonal[...] <= 0, s, MASKED)
            scores[rg % 2, kg] = s
            top = jnp.maximum(top, jnp.max(s.reshape(64, 8, 128), axis=0))
        top = jnp.max(top, axis=0, keepdims=True)
        total = jnp.zeros((8, 128), F32)
        for kg in range(rg + 1):
            e = jnp.exp2(scores[rg % 2, kg] - top)
            scores[rg % 2, kg] = e
            total = total + jnp.sum(e.reshape(64, 8, 128), axis=0)
        inverse = 1.0 / jnp.sum(total, axis=0, keepdims=True)
        acc = jnp.zeros((128, 256), F32)
        for kg in range(rg + 1):
            p = scores[rg % 2, kg] * inverse
            p2 = jnp.concatenate(split(p), axis=1)
            probs[kg, :, lanes] = p2
            scores[rg % 2, kg] = p
            acc = acc + nn(values_t[kg], p2)
        o_t = acc[:, :128] + acc[:, 128:]
        row_delta = jnp.sum(nt(identity, g) * o_t.astype(BF16).astype(F32), axis=0, keepdims=True)
        o_rows[4 * rg : 4 * rg + 4] = o_t.T.reshape(4, 4, 8, 128).astype(BF16)
        acc = jnp.zeros((128, 256), F32)
        for kg in range(rg + 1):
            ds = scores[rg % 2, kg] * (nt(plane_group(1, kg), g) - row_delta)
            ds2 = jnp.concatenate(split(ds), axis=1)
            dscores[kg, :, lanes] = ds2
            acc = acc + nn(keys_t[kg], ds2)
        dq_t = (acc[:, :128] + acc[:, 128:]) * scale
        dq_rows[4 * rg : 4 * rg + 4] = dq_t.T.reshape(4, 4, 8, 128).astype(BF16)

    along = jnp.where(c == 0, x, y)
    across = jnp.where(c == 0, y, x)

    def sibling(kg):
        return pltpu.make_async_remote_copy(
            src_ref=part.at[1 - c, kg], dst_ref=other.at[kg], send_sem=sib_s,
            recv_sem=sib_r.at[kg], device_id=(z, y, x, 1 - c), device_id_type=MESH,
        )

    def row_send(kg, a):
        t = (along + a) & 3
        return pltpu.make_async_remote_copy(
            src_ref=part.at[c, kg, :, t], dst_ref=row_in.at[kg, a - 1], send_sem=row_s,
            recv_sem=row_r.at[kg],
            device_id=(z, jnp.where(c == 0, y, t), jnp.where(c == 0, t, x), c), device_id_type=MESH,
        )

    def block_send(kg, a):
        t = (across + a) & 3
        return pltpu.make_async_remote_copy(
            src_ref=row_sum.at[kg, :, t], dst_ref=block_in.at[kg, a - 1], send_sem=blk_s,
            recv_sem=blk_r.at[kg],
            device_id=(z, jnp.where(c == 0, t, y), jnp.where(c == 0, x, t), c), device_id_type=MESH,
        )

    def combine(kg):
        sibling(kg).wait_recv()
        part[c, kg] = part[c, kg] + other[kg]
        loop(1, 4, lambda a: row_send(kg, a).start())

    with jax.named_scope("p9_trans"):
        for kg in range(4):
            keys_t[kg] = nt(identity, plane_group(0, kg)).astype(BF16)
            values_t[kg] = nt(identity, plane_group(1, kg)).astype(BF16)
    for rg in (3, 2, 1, 0):
        with jax.named_scope(f"p9_rg{rg}"):
            block_of(rg)
            dk = nn(dscores[rg, :, 256 * rg :], q_twice[256 * rg :])
            dv = nn(probs[rg, :, 256 * rg :], g_twice[256 * rg :])
            part[0, rg] = jnp.swapaxes(dk.reshape(4, 4, 4, 8, 128), 1, 2)
            part[1, rg] = dv.reshape(4, 4, 4, 8, 128)
            sibling(rg).start()
        with jax.named_scope(f"pa_comb{rg}"):
            if rg < 3:
                combine(rg + 1)
            loop(4 * rg, 4 * rg + 4, lambda t: (o_start(t), dq_start(t)))

    with jax.named_scope("pb_combine"):
        combine(0)

    def row_finish(i):
        kg = 3 - i
        drain(row_in.at[kg], row_r.at[kg])
        total = part[c, kg, :, along]
        for a in range(3):
            total = total + row_in[kg, a]
        row_sum[kg] = total
        loop(1, 4, lambda a: block_send(kg, a).start())

    factor = jnp.where(c == 0, scale, 1.0).astype(F32)

    def finish(i):
        kg = 3 - i
        drain(block_in.at[kg], blk_r.at[kg])
        total = row_sum[kg, :, across]
        for a in range(3):
            total = total + block_in[kg, a]
        final[pl.ds(4 * kg, 4)] = (total * factor).astype(BF16)

    with jax.named_scope("pc_rows"):
        loop(0, 4, row_finish)
    with jax.named_scope("pc_blocks"):
        loop(0, 4, finish)

    def out(d, other_core):
        t = z_at(d)
        core = 1 - c if other_core else c
        return pltpu.make_async_remote_copy(
            src_ref=final.at[t], dst_ref=dkv_ref.at[c, z], send_sem=fin_s.at[other_core],
            recv_sem=fin_r.at[other_core], device_id=(t, y, x, core), device_id_type=MESH,
        )

    with jax.named_scope("pd_start"):
        loop(1, 16, lambda d: (out(d, 0).start(), out(d, 1).start()))
        out(0, 1).start()
        dkv_ref[c, z] = final[z]

    with jax.named_scope("pe_sends"):
        own_kv.wait_send()
        drain(kv_all.at[0, 0, pl.ds(0, 15)], zkv_s)
        drain(q_rows.at[pl.ds(0, 15)], zq_s)
        drain(g_rows.at[pl.ds(0, 15)], zg_s)
        drain(kv_all.at[0, :, pl.ds(0, 15)], ag_s)
        drain(kv_all.at[0], fw_s)
        o_finish()
        dq_finish()
        drain(other, sib_s)
        drain(row_in, row_s)
        drain(block_in, blk_s)
    with jax.named_scope("pf_dkv"):
        drain(dkv_ref.at[0, pl.ds(0, 15)], fin_s.at[0])
        drain(dkv_ref.at[0], fin_s.at[1])
        drain(dkv_ref.at[0, pl.ds(0, 15)], fin_r.at[0])
        drain(dkv_ref.at[1], fin_r.at[1])


def on_device(q, k, v, g):
    core = lax.axis_index("c")
    wide = (2, 4, 8, 8, 128)
    dma = pltpu.SemaphoreType.DMA
    hbm = pl.BlockSpec(memory_space=pltpu.MemorySpace.HBM)
    vmem = pl.BlockSpec(memory_space=pltpu.VMEM)
    o, dq, dkv = pl.pallas_call(
        kernel,
        out_shape=(
            jax.ShapeDtypeStruct(wide, BF16),
            jax.ShapeDtypeStruct(wide, BF16),
            jax.ShapeDtypeStruct((2, 16, 8, 128), BF16),
        ),
        in_specs=[hbm, hbm, hbm, hbm],
        out_specs=(hbm, hbm, vmem),
        scratch_shapes=[
            pltpu.VMEM(wide, BF16),
            pltpu.VMEM((2, 4, 8, 128), BF16),
            pltpu.VMEM((2, 4, 8, 128), BF16),
            pltpu.VMEM(wide, BF16),
            pltpu.VMEM((2, 8, 8, 128), F32),
            pltpu.VMEM((2, 8, 8, 128), BF16),
            pltpu.VMEM((16, 4, 8, 128), BF16),
            pltpu.VMEM((16, 4, 8, 128), BF16),
            pltpu.VMEM((2, 16, 16, 8, 128), BF16),
            pltpu.VMEM((8, 128), BF16),
            pltpu.VMEM((4, 128, 512), BF16),
            pltpu.VMEM((4, 128, 512), BF16),
            pltpu.VMEM((512, 128), jnp.int32),
            pltpu.VMEM((2, 4, 512, 128), F32),
            pltpu.VMEM((4, 512, 1024), BF16),
            pltpu.VMEM((4, 512, 1024), BF16),
            pltpu.VMEM((1024, 128), BF16),
            pltpu.VMEM((1024, 128), BF16),
            pltpu.VMEM((16, 4, 8, 128), BF16),
            pltpu.VMEM((16, 4, 8, 128), BF16),
            pltpu.VMEM((2, 4, 4, 4, 4, 8, 128), F32),
            pltpu.VMEM((4, 4, 4, 4, 8, 128), F32),
            pltpu.VMEM((4, 3, 4, 4, 8, 128), F32),
            pltpu.VMEM((4, 4, 4, 8, 128), F32),
            pltpu.VMEM((4, 3, 4, 8, 128), F32),
            pltpu.VMEM((16, 8, 128), BF16),
            dma((6,)),
            dma, dma((2,)), dma, dma, dma, dma, dma, dma,
            dma, dma((2, 16)), dma, dma((2,)),
            dma, dma, dma, dma, dma, dma,
            dma, dma((4,)), dma, dma((4,)), dma, dma((4,)), dma((2,)), dma((2,)),
        ],
        compiler_params=pltpu.CompilerParams(
            collective_id=1, has_side_effects=True, vmem_limit_bytes=67043328
        ),
        name="attend",
    )(q.reshape(wide), k, v, g.reshape(wide))
    dkv = lax.dynamic_slice_in_dim(dkv.reshape(2, 2, 8, 8, 128), 4 * core, 4, 3)
    dkv = dkv.transpose(0, 1, 3, 2, 4)
    return o.reshape(q.shape), dq.reshape(q.shape), dkv[0], dkv[1]


def solution(mesh):
    grid = Mesh(mesh.devices.reshape(NZ, NY, NX, 2), ("z", "y", "x", "c"))
    spec = P(None, ("z", "y", "x", "c"), None, None)
    return jax.shard_map(
        on_device, mesh=grid, in_specs=(spec,) * 4, out_specs=(spec,) * 4, check_vma=False
    )
```

time: 77.6 us -> 67.8 us (0.87)
  Pallas kernels: 73.6 us -> 63.6 us
    pallas_call x1, Pallas kernels: 73.6 us -> 63.6 us  [on_device(): pl.pallas_call(kernel, out_shape=(jax.ShapeDtypeStruct(wide, BF16), jax.S...]
where the time goes in v4:
time: 67.8 us; the launch traced here: 67.4 us
  Pallas kernels  63.6 us (94%)
  local copies, waits for them, and re-layouts  3.13 us (5%)
    pallas_call x1, Pallas kernels, on_device(): pl.pallas_call(kernel, out_shape=(jax.ShapeDtypeStruct(wide, BF16), jax.S...  63.6 us
    unnamed x7, local copies, waits for them, and re-layouts  1.62 us

profile of v4, /device:TPU:1, one launch (start us, length us, event | category | flops | bytes accessed | tf_op | source)
XLA Modules:
  0.0 67.4 jit_solution(17712072062462880800)
XLA Ops:
  0.6 63.6 %attend.1 = (bf16[2,4,8,8,128]{4,3,2,1,0:T(8,128)(2,1)}, bf16[2,4,8,8,128]{4,3,2,1,0:T(8,128)(2,1)}, bf16[2,16,8,128]{3,2,1,0:T(8,128)(2,1)}) custom-call(bf16[2,4,8,8,128]{4,3,2,1,0:T(8,128)(2,1)} %bitcast.12, bf16[2,4,8,128]{3,2,1,0:T(8,128)(2,1)} %k_hbm.1, bf16[2,4,8,128]{3,2,1,0:T(8,128)(2,1)} %v_hbm.1, bf16[2,4,8,8,128]{4,3,2,1,0:T(8,128)(2,1)} %bitcast.13), custom_call_target="tpu_custom_call" | custom-call | tf_op jit(solution)/shard_map/attend/pallas_call | solution.py:376
  64.3 0.0 copy-start.1
  64.3 0.9 %constant_dynamic-slice_fusion = bf16[2,2,8,4,128]{4,3,2,1,0:T(4,128)(2,1)S(1)} fusion(bf16[2,2,8,8,128]{4,3,2,1,0:T(8,128)(2,1)} %bitcast.17, s32[]{:T(128)S(6)} %select_n.3), kind=kLoop, calls=%fused_computation.3 | loop fusion | bytes 65540 | tf_op jit(solution)/shard_map/dynamic_slice | solution.py:423
  65.2 0.6 slice_bitcast_fusion
  65.8 0.0 copy-done.1
  65.8 0.0 copy-start
  65.8 0.7 copy.14
  66.5 0.3 copy-done
  66.8 0.7 copy.15
  (1 shorter events, 0.0 us)
Async XLA Ops:
  64.3 1.5 %copy-start.1 = (bf16[2,4,8,8,128]{4,3,2,1,0:T(8,128)(2,1)S(1)}, bf16[2,4,8,8,128]{4,3,2,1,0:T(8,128)(2,1)}, u32[]{:S(2)}) copy-start(bf16[2,4,8,8,128]{4,3,2,1,0:T(8,128)(2,1)} %get-tuple-element.7) | copy-start | bytes 393220
  65.8 1.0 %copy-start = (bf16[2,4,8,8,128]{4,3,2,1,0:T(8,128)(2,1)S(1)}, bf16[2,4,8,8,128]{4,3,2,1,0:T(8,128)(2,1)}, u32[]{:S(2)}) copy-start(bf16[2,4,8,8,128]{4,3,2,1,0:T(8,128)(2,1)} %get-tuple-element.8) | copy-start | bytes 393220

commit v5 on v4

--- a/solution.py
+++ b/solution.py
@@ -31,7 +31,7 @@
 def kernel(
     q_hbm, k_hbm, v_hbm, g_hbm, o_hbm, dq_hbm, dkv_ref,
     q_home, k_home, v_home, g_home, kv_wide, kv_home, q_rows, g_rows, kv_all,
-    mate, keys_t, values_t, diagonal, scores, probs, dscores, g_twice, q_twice,
+    mate, keys_t, values_t, diagonal, row_delta, scores, probs, dscores, g_twice, q_twice,
     o_rows, dq_rows, part, other, row_in, row_sum, block_in, final,
     in_sem, zkv_s, zkv_r, own_s, own_r, zq_s, zq_r, zg_s, zg_r, ag_s, ag_r, fw_s, fw_r,
     o_s, o_r, own_o, dq_s, dq_r, own_dq, sib_s, sib_r, row_s, row_r, blk_s, blk_r, fin_s, fin_r,
@@ -138,9 +138,8 @@
             to_core(0, d, far).start()
             to_core(1, d, far).start()
 
+        loop(1, 5, lambda d: (send_kv(d, 0), send_kv(16 - d, 0)))
         loop(5, 12, lambda d: send_kv(d, 1))
-        loop(1, 5, lambda d: send_kv(d, 0))
-        loop(12, 16, lambda d: send_kv(d, 0))
         loop(1, 16, lambda d: zq(d).start())
         loop(1, 16, lambda d: zg(d).start())
 
@@ -203,13 +202,9 @@
                 recv_sem=recv, device_id=(t, y, x, c), device_id_type=MESH,
             )
         own = pltpu.make_async_copy(rows.at[z], out.at[layer, :, group], own_sem)
-        def start(t):
-            @pl.when(t != z)
-            def _():
-                make(t).start()
-            @pl.when(t == z)
-            def _():
-                own.start()
+        def start():
+            loop(1, 16, lambda d: make(z_at(d)).start())
+            own.start()
         def finish():
             drain(rows.at[pl.ds(0, 15)], send)
             drain(rows.at[pl.ds(0, 15)], recv)
@@ -221,61 +216,79 @@
 
     factor_2 = scale * 1.4426950408889634
 
-    def block_of(rg):
+    def pair(rg):
+        return slice(256 * rg, 256 * rg + 128), slice(256 * rg, 256 * rg + 256)
+
+    def forward_of(rg):
+        first, lanes = pair(rg)
         q = q_rows[4 * rg : 4 * rg + 4].astype(F32).reshape(128, 128).astype(BF16)
         g = g_rows[4 * rg : 4 * rg + 4].astype(F32).reshape(128, 128).astype(BF16)
-        for twice, value in ((q_twice, q), (g_twice, g)):
-            twice[256 * rg : 256 * rg + 128] = value
-            twice[256 * rg + 128 : 256 * rg + 256] = value
-        lanes = slice(256 * rg, 256 * rg + 256)
+        q_twice[lanes] = jnp.concatenate([q, q], axis=0)
+        g_twice[lanes] = jnp.concatenate([g, g], axis=0)
         top = jnp.full((8, 128), MASKED, F32)
         for kg in range(rg + 1):
             s = nt(plane_group(0, kg), q) * factor_2
             if kg == rg:
                 s = jnp.where(diagonal[...] <= 0, s, MASKED)
-            scores[rg % 2, kg] = s
+            scores[rg, kg] = s
             top = jnp.maximum(top, jnp.max(s.reshape(64, 8, 128), axis=0))
         top = jnp.max(top, axis=0, keepdims=True)
         total = jnp.zeros((8, 128), F32)
         for kg in range(rg + 1):
-            e = jnp.exp2(scores[rg % 2, kg] - top)
-            scores[rg % 2, kg] = e
+            e = jnp.exp2(scores[rg, kg] - top)
+            scores[rg, kg] = e
             total = total + jnp.sum(e.reshape(64, 8, 128), axis=0)
         inverse = 1.0 / jnp.sum(total, axis=0, keepdims=True)
         acc = jnp.zeros((128, 256), F32)
         for kg in range(rg + 1):
-            p = scores[rg % 2, kg] * inverse
+            p = scores[rg, kg] * inverse
             p2 = jnp.concatenate(split(p), axis=1)
             probs[kg, :, lanes] = p2
-            scores[rg % 2, kg] = p
+            scores[rg, kg] = p
             acc = acc + nn(values_t[kg], p2)
         o_t = acc[:, :128] + acc[:, 128:]
-        row_delta = jnp.sum(nt(identity, g) * o_t.astype(BF16).astype(F32), axis=0, keepdims=True)
+        delta = nt(identity, g) * o_t.astype(BF16).astype(F32)
+        row_delta[rg : rg + 1] = jnp.sum(delta, axis=0, keepdims=True)
         o_rows[4 * rg : 4 * rg + 4] = o_t.T.reshape(4, 4, 8, 128).astype(BF16)
+
+    def backward_of(rg):
+        first, lanes = pair(rg)
+        g = g_twice[first]
+        delta = row_delta[rg : rg + 1]
         acc = jnp.zeros((128, 256), F32)
         for kg in range(rg + 1):
-            ds = scores[rg % 2, kg] * (nt(plane_group(1, kg), g) - row_delta)
+            ds = scores[rg, kg] * (nt(plane_group(1, kg), g) - delta)
             ds2 = jnp.concatenate(split(ds), axis=1)
             dscores[kg, :, lanes] = ds2
             acc = acc + nn(keys_t[kg], ds2)
         dq_t = (acc[:, :128] + acc[:, 128:]) * scale
         dq_rows[4 * rg : 4 * rg + 4] = dq_t.T.reshape(4, 4, 8, 128).astype(BF16)
 
-    along = jnp.where(c == 0, x, y)
-    across = jnp.where(c == 0, y, x)
+    def value_sum(kg, low, high):
+        lanes = slice(256 * low, 256 * high)
+        return nn(probs[kg, :, lanes], g_twice[lanes]).reshape(4, 4, 4, 8, 128)
+
+    def key_sum(kg, low, high):
+        lanes = slice(256 * low, 256 * high)
+        dk = nn(dscores[kg, :, lanes], q_twice[lanes])
+        return jnp.swapaxes(dk.reshape(4, 4, 4, 8, 128), 1, 2)
+
+    kind = 1 - c
+    along = jnp.where(c == 0, y, x)
+    across = jnp.where(c == 0, x, y)
 
     def sibling(kg):
         return pltpu.make_async_remote_copy(
-            src_ref=part.at[1 - c, kg], dst_ref=other.at[kg], send_sem=sib_s,
+            src_ref=part.at[c, kg], dst_ref=other.at[kg], send_sem=sib_s,
             recv_sem=sib_r.at[kg], device_id=(z, y, x, 1 - c), device_id_type=MESH,
         )
 
     def row_send(kg, a):
         t = (along + a) & 3
         return pltpu.make_async_remote_copy(
-            src_ref=part.at[c, kg, :, t], dst_ref=row_in.at[kg, a - 1], send_sem=row_s,
+            src_ref=part.at[kind, kg, :, t], dst_ref=row_in.at[kg, a - 1], send_sem=row_s,
             recv_sem=row_r.at[kg],
-            device_id=(z, jnp.where(c == 0, y, t), jnp.where(c == 0, t, x), c), device_id_type=MESH,
+            device_id=(z, jnp.where(c == 0, t, y), jnp.where(c == 0, x, t), c), device_id_type=MESH,
         )
 
     def block_send(kg, a):
@@ -283,44 +296,67 @@
         return pltpu.make_async_remote_copy(
             src_ref=row_sum.at[kg, :, t], dst_ref=block_in.at[kg, a - 1], send_sem=blk_s,
             recv_sem=blk_r.at[kg],
-            device_id=(z, jnp.where(c == 0, t, y), jnp.where(c == 0, x, t), c), device_id_type=MESH,
+            device_id=(z, jnp.where(c == 0, y, t), jnp.where(c == 0, t, x), c), device_id_type=MESH,
         )
 
     def combine(kg):
         sibling(kg).wait_recv()
-        part[c, kg] = part[c, kg] + other[kg]
+        part[kind, kg] = part[kind, kg] + other[kg]
         loop(1, 4, lambda a: row_send(kg, a).start())
 
-    with jax.named_scope("p9_trans"):
+    with jax.named_scope("p9_fwd"):
         for kg in range(4):
             keys_t[kg] = nt(identity, plane_group(0, kg)).astype(BF16)
             values_t[kg] = nt(identity, plane_group(1, kg)).astype(BF16)
-    for rg in (3, 2, 1, 0):
-        with jax.named_scope(f"p9_rg{rg}"):
-            block_of(rg)
-            dk = nn(dscores[rg, :, 256 * rg :], q_twice[256 * rg :])
-            dv = nn(probs[rg, :, 256 * rg :], g_twice[256 * rg :])
-            part[0, rg] = jnp.swapaxes(dk.reshape(4, 4, 4, 8, 128), 1, 2)
-            part[1, rg] = dv.reshape(4, 4, 4, 8, 128)
-            sibling(rg).start()
-        with jax.named_scope(f"pa_comb{rg}"):
+        for rg in (3, 2, 1, 0):
+            forward_of(rg)
             if rg < 3:
-                combine(rg + 1)
-            loop(4 * rg, 4 * rg + 4, lambda t: (o_start(t), dq_start(t)))
-
-    with jax.named_scope("pb_combine"):
-        combine(0)
+                part[1, rg + 1] = value_sum(rg + 1, rg + 1, 4)
+        part[1, 0] = value_sum(0, 0, 4)
+
+    def of_core(core, body):
+        @pl.when(c == core)
+        def _():
+            body()
+
+    with jax.named_scope("pa_osend"):
+        of_core(1, lambda: loop(0, 4, lambda i: sibling(3 - i).start()))
+        o_start()
+    with jax.named_scope("p9_bwd3"):
+        backward_of(3)
+        part[0, 3] = key_sum(3, 3, 4)
+    with jax.named_scope("pa_comb3"):
+        of_core(0, lambda: (sibling(3).start(), loop(0, 4, lambda i: combine(3 - i))))
+    with jax.named_scope("p9_bwd2"):
+        backward_of(2)
+        part[0, 2] = key_sum(2, 2, 4)
+    with jax.named_scope("pa_comb2"):
+        of_core(0, lambda: sibling(2).start())
+        of_core(1, lambda: combine(3))
+    with jax.named_scope("p9_bwd1"):
+        backward_of(1)
+        part[0, 1] = key_sum(1, 1, 4)
+    with jax.named_scope("pa_comb1"):
+        of_core(0, lambda: sibling(1).start())
+        of_core(1, lambda: combine(2))
+    with jax.named_scope("p9_bwd0"):
+        backward_of(0)
+        part[0, 0] = key_sum(0, 0, 4)
+    with jax.named_scope("pa_comb0"):
+        of_core(0, lambda: sibling(0).start())
+        dq_start()
+        of_core(1, lambda: (combine(1), combine(0)))
 
     def row_finish(i):
         kg = 3 - i
         drain(row_in.at[kg], row_r.at[kg])
-        total = part[c, kg, :, along]
+        total = part[kind, kg, :, along]
         for a in range(3):
             total = total + row_in[kg, a]
         row_sum[kg] = total
         loop(1, 4, lambda a: block_send(kg, a).start())
 
-    factor = jnp.where(c == 0, scale, 1.0).astype(F32)
+    factor = jnp.where(c == 0, 1.0, scale).astype(F32)
 
     def finish(i):
         kg = 3 - i
@@ -339,14 +375,14 @@
         t = z_at(d)
         core = 1 - c if other_core else c
         return pltpu.make_async_remote_copy(
-            src_ref=final.at[t], dst_ref=dkv_ref.at[c, z], send_sem=fin_s.at[other_core],
+            src_ref=final.at[t], dst_ref=dkv_ref.at[kind, z], send_sem=fin_s.at[other_core],
             recv_sem=fin_r.at[other_core], device_id=(t, y, x, core), device_id_type=MESH,
         )
 
     with jax.named_scope("pd_start"):
         loop(1, 16, lambda d: (out(d, 0).start(), out(d, 1).start()))
         out(0, 1).start()
-        dkv_ref[c, z] = final[z]
+        dkv_ref[kind, z] = final[z]
 
     with jax.named_scope("pe_sends"):
         own_kv.wait_send()
@@ -396,7 +432,8 @@
             pltpu.VMEM((4, 128, 512), BF16),
             pltpu.VMEM((4, 128, 512), BF16),
             pltpu.VMEM((512, 128), jnp.int32),
-            pltpu.VMEM((2, 4, 512, 128), F32),
+            pltpu.VMEM((8, 128), F32),
+            pltpu.VMEM((4, 4, 512, 128), F32),
             pltpu.VMEM((4, 512, 1024), BF16),
             pltpu.VMEM((4, 512, 1024), BF16),
             pltpu.VMEM((1024, 128), BF16),

time: 67.8 us -> 70.8 us (1.044)
  Pallas kernels: 63.6 us -> 66.8 us
    pallas_call x1, Pallas kernels: 63.6 us -> 66.8 us  [on_device(): pl.pallas_call(kernel, out_shape=(jax.ShapeDtypeStruct(wide, BF16), jax.S...]
where the time goes in v5:
time: 70.8 us; the launch traced here: 70.6 us
  Pallas kernels  66.8 us (94%)
  local copies, waits for them, and re-layouts  3.13 us (4%)
    pallas_call x1, Pallas kernels, on_device(): pl.pallas_call(kernel, out_shape=(jax.ShapeDtypeStruct(wide, BF16), jax.S...  66.8 us
    unnamed x7, local copies, waits for them, and re-layouts  1.62 us

profile of v5, /device:TPU:1, one launch (start us, length us, event | category | flops | bytes accessed | tf_op | source)
XLA Modules:
  0.0 70.6 jit_solution(16226177662202321120)
XLA Ops:
  0.6 66.8 %attend.1 = (bf16[2,4,8,8,128]{4,3,2,1,0:T(8,128)(2,1)}, bf16[2,4,8,8,128]{4,3,2,1,0:T(8,128)(2,1)}, bf16[2,16,8,128]{3,2,1,0:T(8,128)(2,1)}) custom-call(bf16[2,4,8,8,128]{4,3,2,1,0:T(8,128)(2,1)} %bitcast.12, bf16[2,4,8,128]{3,2,1,0:T(8,128)(2,1)} %k_hbm.1, bf16[2,4,8,128]{3,2,1,0:T(8,128)(2,1)} %v_hbm.1, bf16[2,4,8,8,128]{4,3,2,1,0:T(8,128)(2,1)} %bitcast.13), custom_call_target="tpu_custom_call" | custom-call | tf_op jit(solution)/shard_map/attend/pallas_call | solution.py:412
  67.4 0.0 copy-start.1
  67.4 0.9 %constant_dynamic-slice_fusion = bf16[2,2,8,4,128]{4,3,2,1,0:T(4,128)(2,1)S(1)} fusion(bf16[2,2,8,8,128]{4,3,2,1,0:T(8,128)(2,1)} %bitcast.17, s32[]{:T(128)S(6)} %select_n.3), kind=kLoop, calls=%fused_computation.3 | loop fusion | bytes 65540 | tf_op jit(solution)/shard_map/dynamic_slice | solution.py:460
  68.4 0.6 slice_bitcast_fusion
  69.0 0.0 copy-done.1
  69.0 0.0 copy-start
  69.0 0.7 copy.14
  69.6 0.3 copy-done
  69.9 0.7 copy.15
  (1 shorter events, 0.0 us)
Async XLA Ops:
  67.4 1.5 %copy-start.1 = (bf16[2,4,8,8,128]{4,3,2,1,0:T(8,128)(2,1)S(1)}, bf16[2,4,8,8,128]{4,3,2,1,0:T(8,128)(2,1)}, u32[]{:S(2)}) copy-start(bf16[2,4,8,8,128]{4,3,2,1,0:T(8,128)(2,1)} %get-tuple-element.7) | copy-start | bytes 393220
  69.0 1.0 %copy-start = (bf16[2,4,8,8,128]{4,3,2,1,0:T(8,128)(2,1)S(1)}, bf16[2,4,8,8,128]{4,3,2,1,0:T(8,128)(2,1)}, u32[]{:S(2)}) copy-start(bf16[2,4,8,8,128]{4,3,2,1,0:T(8,128)(2,1)} %get-tuple-element.8) | copy-start | bytes 393220

commit v6 on v5

--- a/solution.py
+++ b/solution.py
@@ -31,7 +31,7 @@
 def kernel(
     q_hbm, k_hbm, v_hbm, g_hbm, o_hbm, dq_hbm, dkv_ref,
     q_home, k_home, v_home, g_home, kv_wide, kv_home, q_rows, g_rows, kv_all,
-    mate, keys_t, values_t, diagonal, row_delta, scores, probs, dscores, g_twice, q_twice,
+    mate, keys_t, values_t, diagonal, row_delta, attended_t, dq_t, scores, probs, dscores, g_twice, q_twice,
     o_rows, dq_rows, part, other, row_in, row_sum, block_in, final,
     in_sem, zkv_s, zkv_r, own_s, own_r, zq_s, zq_r, zg_s, zg_r, ag_s, ag_r, fw_s, fw_r,
     o_s, o_r, own_o, dq_s, dq_r, own_dq, sib_s, sib_r, row_s, row_r, blk_s, blk_r, fin_s, fin_r,
@@ -193,7 +193,6 @@
 
     with jax.named_scope("p8_qwait"):
         drain(q_rows.at[pl.ds(0, 15)], zq_r)
-        drain(g_rows.at[pl.ds(0, 15)], zg_r)
 
     def home(rows, out, send, recv, own_sem):
         def make(t):
@@ -205,26 +204,31 @@
         def start():
             loop(1, 16, lambda d: make(z_at(d)).start())
             own.start()
+        def start_at(t):
+            @pl.when(t != z)
+            def _():
+                make(t).start()
+            @pl.when(t == z)
+            def _():
+                own.start()
         def finish():
             drain(rows.at[pl.ds(0, 15)], send)
             drain(rows.at[pl.ds(0, 15)], recv)
             own.wait()
-        return start, finish
-
-    o_start, o_finish = home(o_rows, o_hbm, o_s, o_r, own_o)
-    dq_start, dq_finish = home(dq_rows, dq_hbm, dq_s, dq_r, own_dq)
+        return start, start_at, finish
+
+    o_start, _, o_finish = home(o_rows, o_hbm, o_s, o_r, own_o)
+    _, dq_start, dq_finish = home(dq_rows, dq_hbm, dq_s, dq_r, own_dq)
 
     factor_2 = scale * 1.4426950408889634
 
     def pair(rg):
-        return slice(256 * rg, 256 * rg + 128), slice(256 * rg, 256 * rg + 256)
+        return slice(256 * rg, 256 * rg + 256)
 
     def forward_of(rg):
-        first, lanes = pair(rg)
+        lanes = pair(rg)
         q = q_rows[4 * rg : 4 * rg + 4].astype(F32).reshape(128, 128).astype(BF16)
-        g = g_rows[4 * rg : 4 * rg + 4].astype(F32).reshape(128, 128).astype(BF16)
         q_twice[lanes] = jnp.concatenate([q, q], axis=0)
-        g_twice[lanes] = jnp.concatenate([g, g], axis=0)
         top = jnp.full((8, 128), MASKED, F32)
         for kg in range(rg + 1):
             s = nt(plane_group(0, kg), q) * factor_2
@@ -247,22 +251,27 @@
             scores[rg, kg] = p
             acc = acc + nn(values_t[kg], p2)
         o_t = acc[:, :128] + acc[:, 128:]
-        delta = nt(identity, g) * o_t.astype(BF16).astype(F32)
+        attended_t[rg] = o_t.astype(BF16).astype(F32)
+        o_rows[4 * rg : 4 * rg + 4] = o_t.T.reshape(4, 4, 8, 128).astype(BF16)
+
+    def deltas(rg):
+        g = g_rows[4 * rg : 4 * rg + 4].astype(F32).reshape(128, 128).astype(BF16)
+        g_twice[pair(rg)] = jnp.concatenate([g, g], axis=0)
+        delta = nt(identity, g) * attended_t[rg]
         row_delta[rg : rg + 1] = jnp.sum(delta, axis=0, keepdims=True)
-        o_rows[4 * rg : 4 * rg + 4] = o_t.T.reshape(4, 4, 8, 128).astype(BF16)
-
-    def backward_of(rg):
-        first, lanes = pair(rg)
-        g = g_twice[first]
-        delta = row_delta[rg : rg + 1]
-        acc = jnp.zeros((128, 256), F32)
-        for kg in range(rg + 1):
-            ds = scores[rg, kg] * (nt(plane_group(1, kg), g) - delta)
+
+    def backward_of(kg):
+        for rg in range(kg, 4):
+            g = g_twice[256 * rg : 256 * rg + 128]
+            ds = scores[rg, kg] * (nt(plane_group(1, kg), g) - row_delta[rg : rg + 1])
             ds2 = jnp.concatenate(split(ds), axis=1)
-            dscores[kg, :, lanes] = ds2
-            acc = acc + nn(keys_t[kg], ds2)
-        dq_t = (acc[:, :128] + acc[:, 128:]) * scale
-        dq_rows[4 * rg : 4 * rg + 4] = dq_t.T.reshape(4, 4, 8, 128).astype(BF16)
+            dscores[kg, :, pair(rg)] = ds2
+            term = nn(keys_t[kg], ds2)
+            term = term[:, :128] + term[:, 128:]
+            dq_t[rg] = dq_t[rg] + term if kg else term
+        dq_rows[4 * kg : 4 * kg + 4] = (dq_t[kg] * scale).T.reshape(4, 4, 8, 128).astype(BF16)
+        part[0, kg] = key_sum(kg, kg, 4)
+        part[1, kg] = value_sum(kg, kg, 4)
 
     def value_sum(kg, low, high):
         lanes = slice(256 * low, 256 * high)
@@ -308,47 +317,27 @@
         for kg in range(4):
             keys_t[kg] = nt(identity, plane_group(0, kg)).astype(BF16)
             values_t[kg] = nt(identity, plane_group(1, kg)).astype(BF16)
-        for rg in (3, 2, 1, 0):
+        for rg in range(4):
             forward_of(rg)
-            if rg < 3:
-                part[1, rg + 1] = value_sum(rg + 1, rg + 1, 4)
-        part[1, 0] = value_sum(0, 0, 4)
-
-    def of_core(core, body):
-        @pl.when(c == core)
-        def _():
-            body()
 
     with jax.named_scope("pa_osend"):
-        of_core(1, lambda: loop(0, 4, lambda i: sibling(3 - i).start()))
         o_start()
-    with jax.named_scope("p9_bwd3"):
-        backward_of(3)
-        part[0, 3] = key_sum(3, 3, 4)
-    with jax.named_scope("pa_comb3"):
-        of_core(0, lambda: (sibling(3).start(), loop(0, 4, lambda i: combine(3 - i))))
-    with jax.named_scope("p9_bwd2"):
-        backward_of(2)
-        part[0, 2] = key_sum(2, 2, 4)
-    with jax.named_scope("pa_comb2"):
-        of_core(0, lambda: sibling(2).start())
-        of_core(1, lambda: combine(3))
-    with jax.named_scope("p9_bwd1"):
-        backward_of(1)
-        part[0, 1] = key_sum(1, 1, 4)
-    with jax.named_scope("pa_comb1"):
-        of_core(0, lambda: sibling(1).start())
-        of_core(1, lambda: combine(2))
-    with jax.named_scope("p9_bwd0"):
-        backward_of(0)
-        part[0, 0] = key_sum(0, 0, 4)
-    with jax.named_scope("pa_comb0"):
-        of_core(0, lambda: sibling(0).start())
-        dq_start()
-        of_core(1, lambda: (combine(1), combine(0)))
-
-    def row_finish(i):
-        kg = 3 - i
+        drain(g_rows.at[pl.ds(0, 15)], zg_r)
+    for kg in range(4):
+        with jax.named_scope(f"p9_bwd{kg}"):
+            if kg == 0:
+                for rg in range(4):
+                    deltas(rg)
+            backward_of(kg)
+        with jax.named_scope(f"pa_comb{kg}"):
+            sibling(kg).start()
+            loop(4 * kg, 4 * kg + 4, dq_start)
+            if kg:
+                combine(kg - 1)
+    with jax.named_scope("pb_combine"):
+        combine(3)
+
+    def row_finish(kg):
         drain(row_in.at[kg], row_r.at[kg])
         total = part[kind, kg, :, along]
         for a in range(3):
@@ -358,31 +347,35 @@
 
     factor = jnp.where(c == 0, 1.0, scale).astype(F32)
 
-    def finish(i):
-        kg = 3 - i
+    def finish(kg):
         drain(block_in.at[kg], blk_r.at[kg])
         total = row_sum[kg, :, across]
         for a in range(3):
             total = total + block_in[kg, a]
         final[pl.ds(4 * kg, 4)] = (total * factor).astype(BF16)
 
-    with jax.named_scope("pc_rows"):
-        loop(0, 4, row_finish)
-    with jax.named_scope("pc_blocks"):
-        loop(0, 4, finish)
-
-    def out(d, other_core):
-        t = z_at(d)
+    def out(t, other_core):
         core = 1 - c if other_core else c
         return pltpu.make_async_remote_copy(
             src_ref=final.at[t], dst_ref=dkv_ref.at[kind, z], send_sem=fin_s.at[other_core],
             recv_sem=fin_r.at[other_core], device_id=(t, y, x, core), device_id_type=MESH,
         )
 
-    with jax.named_scope("pd_start"):
-        loop(1, 16, lambda d: (out(d, 0).start(), out(d, 1).start()))
-        out(0, 1).start()
-        dkv_ref[kind, z] = final[z]
+    def send_out(t):
+        out(t, 1).start()
+        @pl.when(t != z)
+        def _():
+            out(t, 0).start()
+
+    for kg in range(5):
+        if kg < 4:
+            with jax.named_scope(f"pc_row{kg}"):
+                row_finish(kg)
+        if kg > 0:
+            with jax.named_scope(f"pc_blk{kg - 1}"):
+                finish(kg - 1)
+                loop(4 * kg - 4, 4 * kg, send_out)
+    dkv_ref[kind, z] = final[z]
 
     with jax.named_scope("pe_sends"):
         own_kv.wait_send()
@@ -433,6 +426,8 @@
             pltpu.VMEM((4, 128, 512), BF16),
             pltpu.VMEM((512, 128), jnp.int32),
             pltpu.VMEM((8, 128), F32),
+            pltpu.VMEM((4, 128, 128), F32),
+            pltpu.VMEM((4, 128, 128), F32),
             pltpu.VMEM((4, 4, 512, 128), F32),
             pltpu.VMEM((4, 512, 1024), BF16),
             pltpu.VMEM((4, 512, 1024), BF16),

time: 70.8 us -> 62 us (0.88)
  Pallas kernels: 66.8 us -> 58 us
    pallas_call x1, Pallas kernels: 66.8 us -> 58 us  [on_device(): pl.pallas_call(kernel, out_shape=(jax.ShapeDtypeStruct(wide, BF16), jax.S...]
where the time goes in v6:
time: 62 us; the launch traced here: 61.8 us
  Pallas kernels  58 us (94%)
  local copies, waits for them, and re-layouts  3.13 us (5%)
  between operations  0.67 us (1%)
    pallas_call x1, Pallas kernels, on_device(): pl.pallas_call(kernel, out_shape=(jax.ShapeDtypeStruct(wide, BF16), jax.S...  58 us
    unnamed x7, local copies, waits for them, and re-layouts  1.62 us

profile of v6, /device:TPU:1, one launch (start us, length us, event | category | flops | bytes accessed | tf_op | source)
XLA Modules:
  0.0 61.8 jit_solution(7025815533940847008)
XLA Ops:
  0.6 58.0 %attend.1 = (bf16[2,4,8,8,128]{4,3,2,1,0:T(8,128)(2,1)}, bf16[2,4,8,8,128]{4,3,2,1,0:T(8,128)(2,1)}, bf16[2,16,8,128]{3,2,1,0:T(8,128)(2,1)}) custom-call(bf16[2,4,8,8,128]{4,3,2,1,0:T(8,128)(2,1)} %bitcast.12, bf16[2,4,8,128]{3,2,1,0:T(8,128)(2,1)} %k_hbm.1, bf16[2,4,8,128]{3,2,1,0:T(8,128)(2,1)} %v_hbm.1, bf16[2,4,8,8,128]{4,3,2,1,0:T(8,128)(2,1)} %bitcast.13), custom_call_target="tpu_custom_call" | custom-call | tf_op jit(solution)/shard_map/attend/pallas_call | solution.py:405
  58.7 0.0 copy-start.1
  58.7 0.9 %constant_dynamic-slice_fusion = bf16[2,2,8,4,128]{4,3,2,1,0:T(4,128)(2,1)S(1)} fusion(bf16[2,2,8,8,128]{4,3,2,1,0:T(8,128)(2,1)} %bitcast.17, s32[]{:T(128)S(6)} %select_n.3), kind=kLoop, calls=%fused_computation.3 | loop fusion | bytes 65540 | tf_op jit(solution)/shard_map/dynamic_slice | solution.py:455
  59.6 0.6 slice_bitcast_fusion
  60.2 0.0 copy-done.1
  60.2 0.0 copy-start
  60.2 0.7 %copy.14 = bf16[2,4,64,128]{3,2,1,0:T(8,128)(2,1)} copy(bf16[2,4,64,128]{3,2,1,0:T(8,128)(2,1)S(1)} %bitcast.15) | data formatting | bytes 262144
  60.9 0.3 copy-done
  61.2 0.7 %copy.15 = bf16[2,4,64,128]{3,2,1,0:T(8,128)(2,1)} copy(bf16[2,4,64,128]{3,2,1,0:T(8,128)(2,1)S(1)} %bitcast.14) | data formatting | bytes 262144
  (1 shorter events, 0.0 us)
Async XLA Ops:
  58.7 1.5 %copy-start.1 = (bf16[2,4,8,8,128]{4,3,2,1,0:T(8,128)(2,1)S(1)}, bf16[2,4,8,8,128]{4,3,2,1,0:T(8,128)(2,1)}, u32[]{:S(2)}) copy-start(bf16[2,4,8,8,128]{4,3,2,1,0:T(8,128)(2,1)} %get-tuple-element.7) | copy-start | bytes 393220
  60.2 1.0 %copy-start = (bf16[2,4,8,8,128]{4,3,2,1,0:T(8,128)(2,1)S(1)}, bf16[2,4,8,8,128]{4,3,2,1,0:T(8,128)(2,1)}, u32[]{:S(2)}) copy-start(bf16[2,4,8,8,128]{4,3,2,1,0:T(8,128)(2,1)} %get-tuple-element.8) | copy-start | bytes 393220

commit v7 on v6

--- a/solution.py
+++ b/solution.py
@@ -13,6 +13,7 @@
 BF16 = jnp.bfloat16
 NZ, NY, NX = 16, 4, 4
 MASKED = -1e30
+PIECES = ((0, 7), (7, 6), (13, 3))
 
 
 def nt(a, b):
@@ -110,11 +111,14 @@
 
     half = pl.ds(pl.multiple_of(4 * c, 4), 4)
 
+    def slot_of(u):
+        return u + jnp.where(u < 10, 0, jnp.where(u < 13, 3, -3))
+
     def to_core(core, d, far):
         t = z_at(d)
         return pltpu.make_async_remote_copy(
             src_ref=kv_home.at[t >> 3, t & 7, pl.ds(4 * core, 4)],
-            dst_ref=kv_all.at[core, (20 - d) & 15, chip, half],
+            dst_ref=kv_all.at[core, slot_of((19 - d) & 15), chip, half],
             send_sem=zkv_s, recv_sem=zkv_r.at[far],
             device_id=(t, y, x, core), device_id_type=MESH,
         )
@@ -138,15 +142,15 @@
             to_core(0, d, far).start()
             to_core(1, d, far).start()
 
-        loop(1, 5, lambda d: (send_kv(d, 0), send_kv(16 - d, 0)))
-        loop(5, 12, lambda d: send_kv(d, 1))
+        loop(1, 4, lambda d: (send_kv(d, 0), send_kv(16 - d, 0)))
+        loop(4, 7, lambda d: (send_kv(d, 1), send_kv(16 - d, 1)))
+        loop(7, 10, lambda d: send_kv(d, 2))
         loop(1, 16, lambda d: zq(d).start())
         loop(1, 16, lambda d: zg(d).start())
 
-    PIECES = (pl.ds(0, 9), pl.ds(9, 7))
 
     def gather(n, e):
-        block = kv_all.at[c, PIECES[n], chip]
+        block = kv_all.at[c, pl.ds(*PIECES[n]), chip]
         return pltpu.make_async_remote_copy(
             src_ref=block, dst_ref=block, send_sem=ag_s,
             recv_sem=ag_r.at[n, e], device_id=(z, *chip_at(e, 1), c), device_id_type=MESH,
@@ -154,7 +158,7 @@
 
     def forward(n, e):
         yy, xx = chip_at(e, -1)
-        block = kv_all.at[c, PIECES[n], yy * NX + xx]
+        block = kv_all.at[c, pl.ds(*PIECES[n]), yy * NX + xx]
         return pltpu.make_async_remote_copy(
             src_ref=block, dst_ref=block, send_sem=fw_s,
             recv_sem=fw_r.at[n], device_id=(z, y, x, 1 - c), device_id_type=MESH,
@@ -165,14 +169,18 @@
         mine = kv_wide[layer, group]
         theirs = pltpu.roll(mate[...].astype(F32), 4, 0)
         low_half = (lax.broadcasted_iota(jnp.int32, (8, 128), 0) >> 2) == c
-        kv_all[c, 4, chip] = jnp.where(low_half, mine, theirs).astype(BF16)
-        drain(kv_home.at[0], zkv_r.at[0])
+        kv_all[c, 3, chip] = jnp.where(low_half, mine, theirs).astype(BF16)
+        drain(kv_all.at[0, 0, pl.ds(0, 6)], zkv_r.at[0])
         loop(1, 16, lambda e: gather(0, e).start())
         forward(0, 0).start()
-    with jax.named_scope("p3_zkvf"):
-        drain(kv_home.at[0, pl.ds(0, 7)], zkv_r.at[1])
+    with jax.named_scope("p3_zkvm"):
+        drain(kv_all.at[0, 0, pl.ds(0, 6)], zkv_r.at[1])
         loop(1, 16, lambda e: gather(1, e).start())
         forward(1, 0).start()
+    with jax.named_scope("p3_zkvf"):
+        drain(kv_all.at[0, 0, pl.ds(0, 3)], zkv_r.at[2])
+        loop(1, 16, lambda e: gather(2, e).start())
+        forward(2, 0).start()
 
     def pass_on(n, e):
         gather(n, e).wait_recv()
@@ -180,15 +188,17 @@
 
     with jax.named_scope("p4_agnear"):
         loop(1, 16, lambda e: pass_on(0, e))
+    with jax.named_scope("p4_agmid"):
+        loop(1, 16, lambda e: pass_on(1, e))
     with jax.named_scope("p5_agfar"):
-        loop(1, 16, lambda e: pass_on(1, e))
+        loop(1, 16, lambda e: pass_on(2, e))
     with jax.named_scope("p6_fwd"):
-        drain(kv_all.at[1 - c, PIECES[0]], fw_r.at[0])
-        drain(kv_all.at[1 - c, PIECES[1]], fw_r.at[1])
+        for n in range(3):
+            drain(kv_all.at[1 - c, pl.ds(*PIECES[n])], fw_r.at[n])
 
     def plane_group(kind, kg):
         return jnp.concatenate(
-            [kv_all[kind, (4 * kg + i + 20 - z) & 15].reshape(128, 128) for i in range(4)], axis=0
+            [kv_all[kind, slot_of((4 * kg + i + 19 - z) & 15)].reshape(128, 128) for i in range(4)], axis=0
         )
 
     with jax.named_scope("p8_qwait"):
@@ -396,12 +406,37 @@
         drain(dkv_ref.at[1], fin_r.at[1])
 
 
+def deliver(o_ref, dq_ref, dkv_ref, o_hbm, dq_hbm, dk_hbm, dv_hbm, wide, narrow, sem):
+    c = lax.axis_index("c")
+    copies = [
+        pltpu.make_async_copy(o_ref, o_hbm, sem.at[0]),
+        pltpu.make_async_copy(dq_ref, dq_hbm, sem.at[1]),
+        pltpu.make_async_copy(narrow.at[0], dk_hbm, sem.at[2]),
+        pltpu.make_async_copy(narrow.at[1], dv_hbm, sem.at[3]),
+    ]
+    copies[0].start()
+    copies[1].start()
+    wide[...] = dkv_ref[...].astype(F32)
+    for core in range(2):
+        @pl.when(c == core)
+        def _():
+            for kind in range(2):
+                for l in range(2):
+                    for i in range(4):
+                        rows = wide[kind, 8 * l : 8 * l + 8, 4 * core + i, :]
+                        narrow[kind, l, i] = rows.astype(BF16)
+    copies[2].start()
+    copies[3].start()
+    for copy in copies:
+        copy.wait()
+
+
 def on_device(q, k, v, g):
-    core = lax.axis_index("c")
     wide = (2, 4, 8, 8, 128)
     dma = pltpu.SemaphoreType.DMA
     hbm = pl.BlockSpec(memory_space=pltpu.MemorySpace.HBM)
     vmem = pl.BlockSpec(memory_space=pltpu.VMEM)
+    inputs = (q.reshape(wide), k, v, g.reshape(wide))
     o, dq, dkv = pl.pallas_call(
         kernel,
         out_shape=(
@@ -442,19 +477,28 @@
             pltpu.VMEM((4, 3, 4, 8, 128), F32),
             pltpu.VMEM((16, 8, 128), BF16),
             dma((6,)),
-            dma, dma((2,)), dma, dma, dma, dma, dma, dma,
-            dma, dma((2, 16)), dma, dma((2,)),
+            dma, dma((3,)), dma, dma, dma, dma, dma, dma,
+            dma, dma((3, 16)), dma, dma((3,)),
             dma, dma, dma, dma, dma, dma,
             dma, dma((4,)), dma, dma((4,)), dma, dma((4,)), dma((2,)), dma((2,)),
         ],
         compiler_params=pltpu.CompilerParams(
-            collective_id=1, has_side_effects=True, vmem_limit_bytes=67043328
+            collective_id=1, has_side_effects=True, vmem_limit_bytes=48 * 2**20
         ),
         name="attend",
-    )(q.reshape(wide), k, v, g.reshape(wide))
-    dkv = lax.dynamic_slice_in_dim(dkv.reshape(2, 2, 8, 8, 128), 4 * core, 4, 3)
-    dkv = dkv.transpose(0, 1, 3, 2, 4)
-    return o.reshape(q.shape), dq.reshape(q.shape), dkv[0], dkv[1]
+    )(*(pltpu.with_memory_space_constraint(a, pltpu.MemorySpace.HBM) for a in inputs))
+    o, dq, dk, dv = pl.pallas_call(
+        deliver,
+        out_shape=tuple(jax.ShapeDtypeStruct(a.shape, BF16) for a in (o, dq, k, v)),
+        in_specs=[hbm, hbm, vmem],
+        out_specs=(hbm,) * 4,
+        scratch_shapes=[
+            pltpu.VMEM((2, 16, 8, 128), F32), pltpu.VMEM((2, 2, 4, 8, 128), BF16), dma((4,))
+        ],
+        compiler_params=pltpu.CompilerParams(vmem_limit_bytes=8 * 2**20),
+        name="deliver",
+    )(o, dq, dkv)
+    return o.reshape(q.shape), dq.reshape(q.shape), dk, dv
 
 
 def solution(mesh):

time: 62 us -> 59.1 us (0.953)
  local copies, waits for them, and re-layouts: 3.13 us -> 0 us
    unnamed x7 -> x0, local copies, waits for them, and re-layouts: 1.62 us -> none
    dynamic_slice x1 -> x0, local copies, waits for them, and re-layouts: 0.9 us -> none  [on_device(): dkv = lax.dynamic_slice_in_dim(dkv.reshape(2, 2, 8, 8, 128), 4 * core, 4, 3)]
    pallas_call x0 -> x1, Pallas kernels: none -> 0.74 us  [on_device(): pl.pallas_call(deliver, out_shape=tuple((jax.ShapeDtypeStruct(a.shape, BF...]
where the time goes in v7:
time: 59.1 us; the launch traced here: 58.9 us
  Pallas kernels  58.3 us (99%)
  between operations  0.64 us (1%)
    pallas_call x1, Pallas kernels, on_device(): pl.pallas_call(kernel, out_shape=(jax.ShapeDtypeStruct(wide, BF16), jax.S...  57.5 us

profile of v7, /device:TPU:1, one launch (start us, length us, event | category | flops | bytes accessed | tf_op | source)
XLA Modules:
  0.0 58.9 jit_solution(21825165666658019)
XLA Ops:
  0.6 57.5 %attend.1 = (bf16[2,4,8,8,128]{4,3,2,1,0:T(8,128)(2,1)S(1)}, bf16[2,4,8,8,128]{4,3,2,1,0:T(8,128)(2,1)S(1)}, bf16[2,16,8,128]{3,2,1,0:T(8,128)(2,1)S(1)}) custom-call(bf16[2,4,8,8,128]{4,3,2,1,0:T(8,128)(2,1)} %bitcast.4, bf16[2,4,8,128]{3,2,1,0:T(8,128)(2,1)} %k_hbm.1, bf16[2,4,8,128]{3,2,1,0:T(8,128)(2,1)} %v_hbm.1, bf16[2,4,8,8,128]{4,3,2,1,0:T(8,128)(2,1)} %bitcast.5), custom_call_target="tpu_custom_call" | custom-call | tf_op jit(solution)/shard_map/attend/pallas_call | solution.py:440
  58.2 0.7 %deliver.1 = (bf16[2,4,8,8,128]{4,3,2,1,0:T(8,128)(2,1)}, bf16[2,4,8,8,128]{4,3,2,1,0:T(8,128)(2,1)}, bf16[2,4,8,128]{3,2,1,0:T(8,128)(2,1)}, bf16[2,4,8,128]{3,2,1,0:T(8,128)(2,1)}) custom-call(bf16[2,4,8,8,128]{4,3,2,1,0:T(8,128)(2,1)S(1)} %get-tuple-element.11.o_ref, bf16[2,4,8,8,128]{4,3,2,1,0:T(8,128)(2,1)S(1)} %get-tuple-element.12.dq_ref, ...), custom_call_target="tpu_custom_call" | custom-call | tf_op jit(solution)/shard_map/deliver/pallas_call | solution.py:490

commit v8 on v7

--- a/solution.py
+++ b/solution.py
@@ -33,9 +33,9 @@
     q_hbm, k_hbm, v_hbm, g_hbm, o_hbm, dq_hbm, dkv_ref,
     q_home, k_home, v_home, g_home, kv_wide, kv_home, q_rows, g_rows, kv_all,
     mate, keys_t, values_t, diagonal, row_delta, attended_t, dq_t, scores, probs, dscores, g_twice, q_twice,
-    o_rows, dq_rows, part, other, row_in, row_sum, block_in, final,
+    o_rows, dq_rows, part, other, row_in, row_sum, block_in, first_in, final,
     in_sem, zkv_s, zkv_r, own_s, own_r, zq_s, zq_r, zg_s, zg_r, ag_s, ag_r, fw_s, fw_r,
-    o_s, o_r, own_o, dq_s, dq_r, own_dq, sib_s, sib_r, row_s, row_r, blk_s, blk_r, fin_s, fin_r,
+    o_s, o_r, own_o, dq_s, dq_r, own_dq, sib_s, sib_r, row_s, row_r, blk_s, blk_r, dir_s, dir_r, fin_s, fin_r,
 ):
     z, y, x, c = (lax.axis_index(a) for a in ("z", "y", "x", "c"))
     chip = y * NX + x
@@ -136,6 +136,10 @@
             return 0
         lax.fori_loop(low, high, step, 0)
 
+    def far_first(body):
+        loop(1, 9, lambda i: body(9 - i))
+        loop(9, 16, body)
+
     with jax.named_scope("p2_zstart"):
         own_kv.start()
         def send_kv(d, far):
@@ -146,7 +150,7 @@
         loop(4, 7, lambda d: (send_kv(d, 1), send_kv(16 - d, 1)))
         loop(7, 10, lambda d: send_kv(d, 2))
         loop(1, 16, lambda d: zq(d).start())
-        loop(1, 16, lambda d: zg(d).start())
+        far_first(lambda d: zg(d).start())
 
 
     def gather(n, e):
@@ -212,7 +216,7 @@
             )
         own = pltpu.make_async_copy(rows.at[z], out.at[layer, :, group], own_sem)
         def start():
-            loop(1, 16, lambda d: make(z_at(d)).start())
+            far_first(lambda d: make(z_at(d)).start())
             own.start()
         def start_at(t):
             @pl.when(t != z)
@@ -318,10 +322,21 @@
             device_id=(z, jnp.where(c == 0, y, t), jnp.where(c == 0, t, x), c), device_id_type=MESH,
         )
 
+    def direct_send(j):
+        yy, xx = j >> 2, j & 3
+        a, b = jnp.where(c == 0, yy, xx), jnp.where(c == 0, xx, yy)
+        return pltpu.make_async_remote_copy(
+            src_ref=part.at[kind, 0, :, a, b], dst_ref=first_in.at[(j - chip + 15) & 15],
+            send_sem=dir_s, recv_sem=dir_r, device_id=(z, yy, xx, c), device_id_type=MESH,
+        )
+
     def combine(kg):
         sibling(kg).wait_recv()
         part[kind, kg] = part[kind, kg] + other[kg]
-        loop(1, 4, lambda a: row_send(kg, a).start())
+        if kg:
+            loop(1, 4, lambda a: row_send(kg, a).start())
+        else:
+            loop(1, 16, lambda e: direct_send(jnp.where(e - 1 < chip, e - 1, e)).start())
 
     with jax.named_scope("p9_fwd"):
         for kg in range(4):
@@ -357,6 +372,13 @@
 
     factor = jnp.where(c == 0, 1.0, scale).astype(F32)
 
+    def finish_first():
+        drain(first_in, dir_r)
+        total = part[kind, 0, :, along, across]
+        for e in range(15):
+            total = total + first_in[e]
+        final[pl.ds(0, 4)] = (total * factor).astype(BF16)
+
     def finish(kg):
         drain(block_in.at[kg], blk_r.at[kg])
         total = row_sum[kg, :, across]
@@ -377,11 +399,14 @@
         def _():
             out(t, 0).start()
 
-    for kg in range(5):
+    with jax.named_scope("pc_first"):
+        finish_first()
+        loop(0, 4, send_out)
+    for kg in range(1, 5):
         if kg < 4:
             with jax.named_scope(f"pc_row{kg}"):
                 row_finish(kg)
-        if kg > 0:
+        if kg > 1:
             with jax.named_scope(f"pc_blk{kg - 1}"):
                 finish(kg - 1)
                 loop(4 * kg - 4, 4 * kg, send_out)
@@ -397,8 +422,9 @@
         o_finish()
         dq_finish()
         drain(other, sib_s)
-        drain(row_in, row_s)
-        drain(block_in, blk_s)
+        drain(first_in, dir_s)
+        drain(row_in.at[pl.ds(0, 3)], row_s)
+        drain(block_in.at[pl.ds(0, 3)], blk_s)
     with jax.named_scope("pf_dkv"):
         drain(dkv_ref.at[0, pl.ds(0, 15)], fin_s.at[0])
         drain(dkv_ref.at[0], fin_s.at[1])
@@ -475,12 +501,13 @@
             pltpu.VMEM((4, 3, 4, 4, 8, 128), F32),
             pltpu.VMEM((4, 4, 4, 8, 128), F32),
             pltpu.VMEM((4, 3, 4, 8, 128), F32),
+            pltpu.VMEM((15, 4, 8, 128), F32),
             pltpu.VMEM((16, 8, 128), BF16),
             dma((6,)),
             dma, dma((3,)), dma, dma, dma, dma, dma, dma,
             dma, dma((3, 16)), dma, dma((3,)),
             dma, dma, dma, dma, dma, dma,
-            dma, dma((4,)), dma, dma((4,)), dma, dma((4,)), dma((2,)), dma((2,)),
+            dma, dma((4,)), dma, dma((4,)), dma, dma((4,)), dma, dma, dma((2,)), dma((2,)),
         ],
         compiler_params=pltpu.CompilerParams(
             collective_id=1, has_side_effects=True, vmem_limit_bytes=48 * 2**20

time: 59.1 us -> 56.6 us (0.958)
  Pallas kernels: 58.3 us -> 55.7 us
    pallas_call x1, Pallas kernels: 57.5 us -> 55 us  [on_device(): pl.pallas_call(kernel, out_shape=(jax.ShapeDtypeStruct(wide, BF16), jax.S...]
where the time goes in v8:
time: 56.6 us; the launch traced here: 56.4 us
  Pallas kernels  55.7 us (98%)
  between operations  0.64 us (1%)
    pallas_call x1, Pallas kernels, on_device(): pl.pallas_call(kernel, out_shape=(jax.ShapeDtypeStruct(wide, BF16), jax.S...  55 us

profile of v8, /device:TPU:1, one launch (start us, length us, event | category | flops | bytes accessed | tf_op | source)
XLA Modules:
  0.0 56.4 jit_solution(1397365743456727505)
XLA Ops:
  0.6 55.0 %attend.1 = (bf16[2,4,8,8,128]{4,3,2,1,0:T(8,128)(2,1)S(1)}, bf16[2,4,8,8,128]{4,3,2,1,0:T(8,128)(2,1)S(1)}, bf16[2,16,8,128]{3,2,1,0:T(8,128)(2,1)S(1)}) custom-call(bf16[2,4,8,8,128]{4,3,2,1,0:T(8,128)(2,1)} %bitcast.4, bf16[2,4,8,128]{3,2,1,0:T(8,128)(2,1)} %k_hbm.1, bf16[2,4,8,128]{3,2,1,0:T(8,128)(2,1)} %v_hbm.1, bf16[2,4,8,8,128]{4,3,2,1,0:T(8,128)(2,1)} %bitcast.5), custom_call_target="tpu_custom_call" | custom-call | tf_op jit(solution)/shard_map/attend/pallas_call | solution.py:466
  55.6 0.7 %deliver.1 = (bf16[2,4,8,8,128]{4,3,2,1,0:T(8,128)(2,1)}, bf16[2,4,8,8,128]{4,3,2,1,0:T(8,128)(2,1)}, bf16[2,4,8,128]{3,2,1,0:T(8,128)(2,1)}, bf16[2,4,8,128]{3,2,1,0:T(8,128)(2,1)}) custom-call(bf16[2,4,8,8,128]{4,3,2,1,0:T(8,128)(2,1)S(1)} %get-tuple-element.11.o_ref, bf16[2,4,8,8,128]{4,3,2,1,0:T(8,128)(2,1)S(1)} %get-tuple-element.12.dq_ref, ...), custom_call_target="tpu_custom_call" | custom-call | tf_op jit(solution)/shard_map/deliver/pallas_call | solution.py:517

commit v9 on v8

--- a/solution.py
+++ b/solution.py
@@ -32,7 +32,7 @@
 def kernel(
     q_hbm, k_hbm, v_hbm, g_hbm, o_hbm, dq_hbm, dkv_ref,
     q_home, k_home, v_home, g_home, kv_wide, kv_home, q_rows, g_rows, kv_all,
-    mate, keys_t, values_t, diagonal, row_delta, attended_t, dq_t, scores, probs, dscores, g_twice, q_twice,
+    mate, keys_t, values_t, diagonal, row_delta, tops, attended_t, dq_t, scores, probs, dscores, g_twice, q_twice,
     o_rows, dq_rows, part, other, row_in, row_sum, block_in, first_in, final,
     in_sem, zkv_s, zkv_r, own_s, own_r, zq_s, zq_r, zg_s, zg_r, ag_s, ag_r, fw_s, fw_r,
     o_s, o_r, own_o, dq_s, dq_r, own_dq, sib_s, sib_r, row_s, row_r, blk_s, blk_r, dir_s, dir_r, fin_s, fin_r,
@@ -117,8 +117,8 @@
     def to_core(core, d, far):
         t = z_at(d)
         return pltpu.make_async_remote_copy(
-            src_ref=kv_home.at[t >> 3, t & 7, pl.ds(4 * core, 4)],
-            dst_ref=kv_all.at[core, slot_of((19 - d) & 15), chip, half],
+            src_ref=kv_home.at[t >> 3, t & 7, pl.ds(4 - 4 * core, 4)],
+            dst_ref=kv_all.at[1 - core, slot_of((19 - d) & 15), chip, half],
             send_sem=zkv_s, recv_sem=zkv_r.at[far],
             device_id=(t, y, x, core), device_id_type=MESH,
         )
@@ -154,15 +154,14 @@
 
 
     def gather(n, e):
-        block = kv_all.at[c, pl.ds(*PIECES[n]), chip]
+        block = kv_all.at[1 - c, pl.ds(*PIECES[n]), chip]
         return pltpu.make_async_remote_copy(
             src_ref=block, dst_ref=block, send_sem=ag_s,
-            recv_sem=ag_r.at[n, e], device_id=(z, *chip_at(e, 1), c), device_id_type=MESH,
-        )
-
-    def forward(n, e):
-        yy, xx = chip_at(e, -1)
-        block = kv_all.at[c, pl.ds(*PIECES[n]), yy * NX + xx]
+            recv_sem=ag_r.at[n], device_id=(z, *chip_at(e, 1), c), device_id_type=MESH,
+        )
+
+    def forward(n):
+        block = kv_all.at[1 - c, pl.ds(*PIECES[n])]
         return pltpu.make_async_remote_copy(
             src_ref=block, dst_ref=block, send_sem=fw_s,
             recv_sem=fw_r.at[n], device_id=(z, y, x, 1 - c), device_id_type=MESH,
@@ -170,35 +169,33 @@
 
     with jax.named_scope("p3_zkvn"):
         own_kv.wait_recv()
-        mine = kv_wide[layer, group]
-        theirs = pltpu.roll(mate[...].astype(F32), 4, 0)
-        low_half = (lax.broadcasted_iota(jnp.int32, (8, 128), 0) >> 2) == c
-        kv_all[c, 3, chip] = jnp.where(low_half, mine, theirs).astype(BF16)
+        mine = pltpu.roll(kv_wide[layer, group], 4, 0)
+        own_half = (lax.broadcasted_iota(jnp.int32, (8, 128), 0) >> 2) == c
+        kv_all[1 - c, 3, chip] = jnp.where(own_half, mine, mate[...].astype(F32)).astype(BF16)
         drain(kv_all.at[0, 0, pl.ds(0, 6)], zkv_r.at[0])
         loop(1, 16, lambda e: gather(0, e).start())
-        forward(0, 0).start()
     with jax.named_scope("p3_zkvm"):
         drain(kv_all.at[0, 0, pl.ds(0, 6)], zkv_r.at[1])
         loop(1, 16, lambda e: gather(1, e).start())
-        forward(1, 0).start()
     with jax.named_scope("p3_zkvf"):
         drain(kv_all.at[0, 0, pl.ds(0, 3)], zkv_r.at[2])
         loop(1, 16, lambda e: gather(2, e).start())
-        forward(2, 0).start()
-
-    def pass_on(n, e):
-        gather(n, e).wait_recv()
-        forward(n, e).start()
-
-    with jax.named_scope("p4_agnear"):
-        loop(1, 16, lambda e: pass_on(0, e))
-    with jax.named_scope("p4_agmid"):
-        loop(1, 16, lambda e: pass_on(1, e))
-    with jax.named_scope("p5_agfar"):
-        loop(1, 16, lambda e: pass_on(2, e))
-    with jax.named_scope("p6_fwd"):
+
+    for n in range(3):
+        with jax.named_scope(f"p4_ag{n}"):
+            drain(kv_all.at[1 - c, pl.ds(*PIECES[n]), pl.ds(0, 15)], ag_r.at[n])
+            forward(n).start()
+    def of_core(core, body):
+        @pl.when(c == core)
+        def _():
+            body()
+
+    def from_sibling():
         for n in range(3):
-            drain(kv_all.at[1 - c, pl.ds(*PIECES[n])], fw_r.at[n])
+            drain(kv_all.at[c, pl.ds(*PIECES[n])], fw_r.at[n])
+
+    with jax.named_scope("p6_keys"):
+        of_core(0, from_sibling)
 
     def plane_group(kind, kg):
         return jnp.concatenate(
@@ -239,7 +236,7 @@
     def pair(rg):
         return slice(256 * rg, 256 * rg + 256)
 
-    def forward_of(rg):
+    def scores_of(rg):
         lanes = pair(rg)
         q = q_rows[4 * rg : 4 * rg + 4].astype(F32).reshape(128, 128).astype(BF16)
         q_twice[lanes] = jnp.concatenate([q, q], axis=0)
@@ -250,7 +247,10 @@
                 s = jnp.where(diagonal[...] <= 0, s, MASKED)
             scores[rg, kg] = s
             top = jnp.maximum(top, jnp.max(s.reshape(64, 8, 128), axis=0))
-        top = jnp.max(top, axis=0, keepdims=True)
+        return jnp.max(top, axis=0, keepdims=True)
+
+    def forward_of(rg, top):
+        lanes = pair(rg)
         total = jnp.zeros((8, 128), F32)
         for kg in range(rg + 1):
             e = jnp.exp2(scores[rg, kg] - top)
@@ -338,12 +338,18 @@
         else:
             loop(1, 16, lambda e: direct_send(jnp.where(e - 1 < chip, e - 1, e)).start())
 
+    with jax.named_scope("p9_scores"):
+        for rg in range(4):
+            tops[rg : rg + 1] = scores_of(rg)
+        for kg in range(4):
+            keys_t[kg] = nt(identity, plane_group(0, kg)).astype(BF16)
+    with jax.named_scope("p9_values"):
+        of_core(1, from_sibling)
     with jax.named_scope("p9_fwd"):
         for kg in range(4):
-            keys_t[kg] = nt(identity, plane_group(0, kg)).astype(BF16)
             values_t[kg] = nt(identity, plane_group(1, kg)).astype(BF16)
         for rg in range(4):
-            forward_of(rg)
+            forward_of(rg, tops[rg : rg + 1])
 
     with jax.named_scope("pa_osend"):
         o_start()
@@ -402,14 +408,13 @@
     with jax.named_scope("pc_first"):
         finish_first()
         loop(0, 4, send_out)
-    for kg in range(1, 5):
-        if kg < 4:
-            with jax.named_scope(f"pc_row{kg}"):
-                row_finish(kg)
-        if kg > 1:
-            with jax.named_scope(f"pc_blk{kg - 1}"):
-                finish(kg - 1)
-                loop(4 * kg - 4, 4 * kg, send_out)
+    for kg in range(1, 4):
+        with jax.named_scope(f"pc_row{kg}"):
+            row_finish(kg)
+    for kg in range(1, 4):
+        with jax.named_scope(f"pc_blk{kg}"):
+            finish(kg)
+            loop(4 * kg, 4 * kg + 4, send_out)
     dkv_ref[kind, z] = final[z]
 
     with jax.named_scope("pe_sends"):
@@ -487,6 +492,7 @@
             pltpu.VMEM((4, 128, 512), BF16),
             pltpu.VMEM((512, 128), jnp.int32),
             pltpu.VMEM((8, 128), F32),
+            pltpu.VMEM((8, 128), F32),
             pltpu.VMEM((4, 128, 128), F32),
             pltpu.VMEM((4, 128, 128), F32),
             pltpu.VMEM((4, 4, 512, 128), F32),
@@ -505,7 +511,7 @@
             pltpu.VMEM((16, 8, 128), BF16),
             dma((6,)),
             dma, dma((3,)), dma, dma, dma, dma, dma, dma,
-            dma, dma((3, 16)), dma, dma((3,)),
+            dma, dma((3,)), dma, dma((3,)),
             dma, dma, dma, dma, dma, dma,
             dma, dma((4,)), dma, dma((4,)), dma, dma((4,)), dma, dma, dma((2,)), dma((2,)),
         ],

time: 56.6 us -> 56.8 us (level)
  the two profiles are of different devices: /device:TPU:1 before, /device:TPU:48 now
where the time goes in v9:
time: 56.8 us; the launch traced here: 56.6 us
  Pallas kernels  55.9 us (98%)
  between operations  0.64 us (1%)
    pallas_call x1, Pallas kernels, on_device(): pl.pallas_call(kernel, out_shape=(jax.ShapeDtypeStruct(wide, BF16), jax.S...  55.2 us

profile of v9, /device:TPU:48, one launch (start us, length us, event | category | flops | bytes accessed | tf_op | source)
XLA Modules:
  0.0 56.6 jit_solution(5717571212223712331)
XLA Ops:
  0.6 55.2 %attend.1 = (bf16[2,4,8,8,128]{4,3,2,1,0:T(8,128)(2,1)S(1)}, bf16[2,4,8,8,128]{4,3,2,1,0:T(8,128)(2,1)S(1)}, bf16[2,16,8,128]{3,2,1,0:T(8,128)(2,1)S(1)}) custom-call(bf16[2,4,8,8,128]{4,3,2,1,0:T(8,128)(2,1)} %bitcast.4, bf16[2,4,8,128]{3,2,1,0:T(8,128)(2,1)} %k_hbm.1, bf16[2,4,8,128]{3,2,1,0:T(8,128)(2,1)} %v_hbm.1, bf16[2,4,8,8,128]{4,3,2,1,0:T(8,128)(2,1)} %bitcast.5), custom_call_target="tpu_custom_call" | custom-call | tf_op jit(solution)/shard_map/attend/pallas_call | solution.py:471
  55.8 0.7 %deliver.1 = (bf16[2,4,8,8,128]{4,3,2,1,0:T(8,128)(2,1)}, bf16[2,4,8,8,128]{4,3,2,1,0:T(8,128)(2,1)}, bf16[2,4,8,128]{3,2,1,0:T(8,128)(2,1)}, bf16[2,4,8,128]{3,2,1,0:T(8,128)(2,1)}) custom-call(bf16[2,4,8,8,128]{4,3,2,1,0:T(8,128)(2,1)S(1)} %get-tuple-element.11.o_ref, bf16[2,4,8,8,128]{4,3,2,1,0:T(8,128)(2,1)S(1)} %get-tuple-element.12.dq_ref, ...), custom_call_target="tpu_custom_call" | custom-call | tf_op jit(solution)/shard_map/deliver/pallas_call | solution.py:523

commit v10 on v9

--- a/solution.py
+++ b/solution.py
@@ -154,10 +154,11 @@
 
 
     def gather(n, e):
+        j = jnp.where(e - 1 < chip, e - 1, e)
         block = kv_all.at[1 - c, pl.ds(*PIECES[n]), chip]
         return pltpu.make_async_remote_copy(
             src_ref=block, dst_ref=block, send_sem=ag_s,
-            recv_sem=ag_r.at[n], device_id=(z, *chip_at(e, 1), c), device_id_type=MESH,
+            recv_sem=ag_r.at[n], device_id=(z, j >> 2, j & 3, c), device_id_type=MESH,
         )
 
     def forward(n):

time: 56.8 us -> 55.2 us (0.972)
  the two profiles are of different devices: /device:TPU:48 before, /device:TPU:1 now
where the time goes in v10:
time: 55.2 us; the launch traced here: 55 us
  Pallas kernels  54.4 us (99%)
  between operations  0.64 us (1%)
    pallas_call x1, Pallas kernels, on_device(): pl.pallas_call(kernel, out_shape=(jax.ShapeDtypeStruct(wide, BF16), jax.S...  53.7 us

profile of v10, /device:TPU:1, one launch (start us, length us, event | category | flops | bytes accessed | tf_op | source)
XLA Modules:
  0.0 55.0 jit_solution(14850633502828197163)
XLA Ops:
  0.6 53.7 %attend.1 = (bf16[2,4,8,8,128]{4,3,2,1,0:T(8,128)(2,1)S(1)}, bf16[2,4,8,8,128]{4,3,2,1,0:T(8,128)(2,1)S(1)}, bf16[2,16,8,128]{3,2,1,0:T(8,128)(2,1)S(1)}) custom-call(bf16[2,4,8,8,128]{4,3,2,1,0:T(8,128)(2,1)} %bitcast.4, bf16[2,4,8,128]{3,2,1,0:T(8,128)(2,1)} %k_hbm.1, bf16[2,4,8,128]{3,2,1,0:T(8,128)(2,1)} %v_hbm.1, bf16[2,4,8,8,128]{4,3,2,1,0:T(8,128)(2,1)} %bitcast.5), custom_call_target="tpu_custom_call" | custom-call | tf_op jit(solution)/shard_map/attend/pallas_call | solution.py:472
  54.3 0.7 %deliver.1 = (bf16[2,4,8,8,128]{4,3,2,1,0:T(8,128)(2,1)}, bf16[2,4,8,8,128]{4,3,2,1,0:T(8,128)(2,1)}, bf16[2,4,8,128]{3,2,1,0:T(8,128)(2,1)}, bf16[2,4,8,128]{3,2,1,0:T(8,128)(2,1)}) custom-call(bf16[2,4,8,8,128]{4,3,2,1,0:T(8,128)(2,1)S(1)} %get-tuple-element.11.o_ref, bf16[2,4,8,8,128]{4,3,2,1,0:T(8,128)(2,1)S(1)} %get-tuple-element.12.dq_ref, ...), custom_call_target="tpu_custom_call" | custom-call | tf_op jit(solution)/shard_map/deliver/pallas_call | solution.py:524

commit v11 on v10

--- a/solution.py
+++ b/solution.py
@@ -395,8 +395,9 @@
 
     def out(t, other_core):
         core = 1 - c if other_core else c
-        return pltpu.make_async_remote_copy(
-            src_ref=final.at[t], dst_ref=dkv_ref.at[kind, z], send_sem=fin_s.at[other_core],
+        rows = pl.ds(pl.multiple_of(4 * core, 4), 4)
+        return pltpu.make_async_remote_copy(
+            src_ref=final.at[t, rows], dst_ref=dkv_ref.at[kind, z, rows], send_sem=fin_s.at[other_core],
             recv_sem=fin_r.at[other_core], device_id=(t, y, x, core), device_id_type=MESH,
         )
 
@@ -432,10 +433,9 @@
         drain(row_in.at[pl.ds(0, 3)], row_s)
         drain(block_in.at[pl.ds(0, 3)], blk_s)
     with jax.named_scope("pf_dkv"):
-        drain(dkv_ref.at[0, pl.ds(0, 15)], fin_s.at[0])
-        drain(dkv_ref.at[0], fin_s.at[1])
-        drain(dkv_ref.at[0, pl.ds(0, 15)], fin_r.at[0])
-        drain(dkv_ref.at[1], fin_r.at[1])
+        for sem in (fin_s, fin_r):
+            drain(dkv_ref.at[0, pl.ds(0, 15), pl.ds(0, 4)], sem.at[0])
+            drain(dkv_ref.at[1, :, pl.ds(0, 4)], sem.at[1])
 
 
 def deliver(o_ref, dq_ref, dkv_ref, o_hbm, dq_hbm, dk_hbm, dv_hbm, wide, narrow, sem):

time: 55.2 us -> 55.1 us (level)
  no operation moved by 1% of the time
where the time goes in v11:
time: 55.1 us; the launch traced here: 54.9 us
  Pallas kernels  54.3 us (99%)
  between operations  0.64 us (1%)
    pallas_call x1, Pallas kernels, on_device(): pl.pallas_call(kernel, out_shape=(jax.ShapeDtypeStruct(wide, BF16), jax.S...  53.6 us

profile of v11, /device:TPU:1, one launch (start us, length us, event | category | flops | bytes accessed | tf_op | source)
XLA Modules:
  0.0 54.9 jit_solution(5675516650669492872)
XLA Ops:
  0.6 53.6 %attend.1 = (bf16[2,4,8,8,128]{4,3,2,1,0:T(8,128)(2,1)S(1)}, bf16[2,4,8,8,128]{4,3,2,1,0:T(8,128)(2,1)S(1)}, bf16[2,16,8,128]{3,2,1,0:T(8,128)(2,1)S(1)}) custom-call(bf16[2,4,8,8,128]{4,3,2,1,0:T(8,128)(2,1)} %bitcast.4, bf16[2,4,8,128]{3,2,1,0:T(8,128)(2,1)} %k_hbm.1, bf16[2,4,8,128]{3,2,1,0:T(8,128)(2,1)} %v_hbm.1, bf16[2,4,8,8,128]{4,3,2,1,0:T(8,128)(2,1)} %bitcast.5), custom_call_target="tpu_custom_call" | custom-call | tf_op jit(solution)/shard_map/attend/pallas_call | solution.py:472
  54.2 0.7 %deliver.1 = (bf16[2,4,8,8,128]{4,3,2,1,0:T(8,128)(2,1)}, bf16[2,4,8,8,128]{4,3,2,1,0:T(8,128)(2,1)}, bf16[2,4,8,128]{3,2,1,0:T(8,128)(2,1)}, bf16[2,4,8,128]{3,2,1,0:T(8,128)(2,1)}) custom-call(bf16[2,4,8,8,128]{4,3,2,1,0:T(8,128)(2,1)S(1)} %get-tuple-element.11.o_ref, bf16[2,4,8,8,128]{4,3,2,1,0:T(8,128)(2,1)S(1)} %get-tuple-element.12.dq_ref, ...), custom_call_target="tpu_custom_call" | custom-call | tf_op jit(solution)/shard_map/deliver/pallas_call | solution.py:524
